TPU v7x, 32 devices: a whole 2x2x4 slice. The times are simulated.
32 devices in a mesh: dp: 8 (over z, x), expert: 4 (over y, core).
Axes of the slice: x: 2, y: 2, z: 4, core: 2. Of those that a mesh axis runs over, the one named last changes fastest.
Arguments:
- tokens: bfloat16 [4096, 2048], P(('dp', 'expert')), may hold values from -6 to 6
- out_grad: bfloat16 [4096, 2048], P(('dp', 'expert')), may hold values from -3 to 3
- z_weight: float32 [4096], P(('dp', 'expert')), may hold values from 0.1 to 1
- router_weight: bfloat16 [2048, 128], replicated, may hold values from -0.125 to 0.125
- expert_ids: int32 [4096, 4], P(('dp', 'expert')), may hold values from 0 to 127, as said below
- gate_up_weight: bfloat16 [4, 2048, 3072], P('expert'), may hold values from -0.125 to 0.125
- down_weight: bfloat16 [4, 1536, 2048], P('expert'), may hold values from -0.15625 to 0.15625
Outputs:
- token_grad: bfloat16 [4096, 2048], P(('dp', 'expert'))
- router_grad: float32 [2048, 128], replicated
- gate_up_grad: bfloat16 [4, 2048, 3072], P('expert', 'dp')
- down_grad: bfloat16 [4, 1536, 2048], P('expert', 'dp')
Inputs may be any that keep to these rules, and one draw needn't show every extreme that they name: `expert_ids`: each row names 4 different experts. Experts 0 to 3 are the ones in flight. The 128 rows of one device name any one expert in flight at most 64 times; in every data group some expert in flight is named exactly 64 times by the rows of each device of the group.
All inputs are finite; a program needn't handle non-finite values.
Results may differ from a plain program's by a relative error of at most 0.019.
Values may be sent and summed in bfloat16 or wider, within the bound.
A program may use at most 192 MiB of HBM per device.

v0:
```python
import functools

import jax
import jax.numpy as jnp
from jax import lax
from jax.experimental import pallas as pl
from jax.experimental.pallas import tpu as pltpu
from jax.sharding import PartitionSpec as P

F32 = jnp.float32
BF16 = jnp.bfloat16
MESH = pl.DeviceIdType.MESH


def ring_order(count):
    inner = max(k for k in range(1, count + 1) if count % k == 0 and k * k <= count)
    outer = count // inner
    if inner == 1 or outer % 2:
        return list(range(count))
    order = []
    for row in range(outer):
        cols = list(range(1, inner))
        order += [row * inner + col for col in (cols if row % 2 == 0 else cols[::-1])]
    return order + [row * inner for row in range(outer)][::-1]


def lookup(table, key):
    value = jnp.int32(0)
    for slot, entry in enumerate(table):
        value = value + jnp.where(key == slot, jnp.int32(entry), jnp.int32(0))
    return value


def grads_part(
    copies, flight, order, top,
    tok_ref, rw_ref, wg_ref, xt_ref, pg_ref, ht_ref, dy_ref, score_ref, logit_ref, small_ref, spot_ref, back, home_dx,
    gu_ref, dn_ref, rout_ref, tg_ref,
    gu_buf, dn_buf, rx_e, rsum, rx_d, rfull, rp_ref, home_score, lg_ref,
    send_sem, recv_sem, es_send, es_recv, ds_send, ds_recv, dg_send, dg_recv, eg_send, eg_recv,
    dx_send, dx_recv, sc_send, sc_recv,
):
    d = lax.axis_index("dp")
    e = lax.axis_index("expert")
    n = copies
    place = [order.index(i) for i in range(n)]
    pos = lookup(place, d)
    right = lookup(order, lax.rem(pos + 1, n))
    left = lookup(order, lax.rem(pos + n - 1, n))
    towards = (right, left)

    gu_rows = gu_ref.shape[1]
    half_rows = gu_rows // 2
    dn_rows = dn_ref.shape[1]
    gu_cols = gu_ref.shape[2] // 2
    dn_cols = dn_ref.shape[2] // 2
    piece_e = rsum.shape[0]
    piece_d = rx_d.shape[1]

    def owner_at(way, step):
        if way == 0:
            return lookup(order, lax.rem(pos + 2 * n - 1 - step, n))
        return lookup(order, lax.rem(pos + 1 + step, n))

    def own(way, part, owner):
        if part < 2:
            start = pl.multiple_of(owner * gu_rows + part * half_rows, half_rows)
            return jnp.dot(
                xt_ref[pl.ds(start, half_rows), :],
                pg_ref[:, way * gu_cols:(way + 1) * gu_cols],
                preferred_element_type=F32,
            )
        start = pl.multiple_of(owner * dn_rows, dn_rows)
        return jnp.dot(
            ht_ref[pl.ds(start, dn_rows), :],
            dy_ref[:, way * dn_cols:(way + 1) * dn_cols],
            preferred_element_type=F32,
        )

    def slot(way, part, step):
        return gu_buf.at[way, part, step] if part < 2 else dn_buf.at[way, step]

    def hop(way, part, step):
        return pltpu.make_async_remote_copy(
            src_ref=slot(way, part, step),
            dst_ref=slot(way, part, step + 1),
            send_sem=send_sem.at[way, part, step],
            recv_sem=recv_sem.at[way, part, step],
            device_id=(towards[way], e),
            device_id_type=MESH,
        )

    def share_e(k):
        to = lax.rem(e + k, flight)
        return pltpu.make_async_remote_copy(
            src_ref=rp_ref.at[pl.ds(pl.multiple_of(to * piece_e, piece_e), piece_e), :],
            dst_ref=rx_e.at[k - 1],
            send_sem=es_send.at[k - 1], recv_sem=es_recv.at[k - 1],
            device_id=(d, to), device_id_type=MESH,
        )

    def share_d(k):
        to = lax.rem(d + k, n)
        return pltpu.make_async_remote_copy(
            src_ref=rsum.at[pl.ds(pl.multiple_of(to * piece_d, piece_d), piece_d), :],
            dst_ref=rx_d.at[k - 1],
            send_sem=ds_send.at[k - 1], recv_sem=ds_recv.at[k - 1],
            device_id=(to, e), device_id_type=MESH,
        )

    def gather_d(k, source):
        rows = pl.ds(pl.multiple_of(e * piece_e + source * piece_d, piece_d), piece_d)
        return pltpu.make_async_remote_copy(
            src_ref=rfull.at[rows, :], dst_ref=rfull.at[rows, :],
            send_sem=dg_send.at[k - 1], recv_sem=dg_recv.at[k - 1],
            device_id=(lax.rem(d + k, n), e), device_id_type=MESH,
        )

    def gather_e(k, source):
        rows = pl.ds(pl.multiple_of(source * piece_e, piece_e), piece_e)
        return pltpu.make_async_remote_copy(
            src_ref=rfull.at[rows, :], dst_ref=rfull.at[rows, :],
            send_sem=eg_send.at[k - 1], recv_sem=eg_recv.at[k - 1],
            device_id=(d, lax.rem(e + k, flight)), device_id_type=MESH,
        )

    cap = home_score.shape[1]

    def block(ref, index):
        return ref.at[pl.ds(pl.multiple_of(index * cap, cap), cap), :]

    def give_score(k, source):
        to = lax.rem(e + k, flight)
        return pltpu.make_async_remote_copy(
            src_ref=block(score_ref, to), dst_ref=home_score.at[source],
            send_sem=sc_send.at[k - 1], recv_sem=sc_recv.at[k - 1],
            device_id=(d, to), device_id_type=MESH,
        )

    def give_dx(k, source):
        to = lax.rem(e + k, flight)
        return pltpu.make_async_remote_copy(
            src_ref=block(back, to), dst_ref=block(home_dx, source),
            send_sem=dx_send.at[k - 1], recv_sem=dx_recv.at[k - 1],
            device_id=(d, to), device_id_type=MESH,
        )

    def from_peer(k):
        return lax.rem(e + flight - k, flight)

    def one_hot(k):
        spots = lax.broadcasted_iota(jnp.int32, (tok_ref.shape[0], flight * cap), 1)
        return spots == spot_ref[:, k:k + 1]

    for part in range(3):
        for way in range(2):
            slot(way, part, 0)[...] = own(way, part, owner_at(way, 0)).astype(BF16)
            hop(way, part, 0).start()
    for k in range(1, flight):
        give_score(k, e).start()
    home_score[e] = score_ref[pl.ds(pl.multiple_of(e * cap, cap), cap), :]

    width = back.shape[1]
    tile = min(width, 512)
    for col in range(0, width, tile):
        back[:, col:col + tile] = lax.dot_general(
            pg_ref[...], wg_ref[col:col + tile, :], (((1,), (1,)), ((), ())),
            preferred_element_type=F32,
        ).astype(BF16)
    own_rows = pl.ds(pl.multiple_of(e * cap, cap), cap)
    home_dx[own_rows, :] = back[own_rows, :]

    def middle(step, carry):
        for part in range(3):
            for way in range(2):
                hop(way, part, step - 1).wait_recv()
                here = slot(way, part, step)
                here[...] = (
                    here[...].astype(F32) + own(way, part, owner_at(way, step))
                ).astype(BF16)
                hop(way, part, step).start()

        @pl.when(step == 1)
        def _():
            for k in range(1, flight):
                give_score(k, from_peer(k)).wait_recv()
            for k in range(1, flight):
                give_dx(k, e).start()
            arrived = home_score[...].reshape(flight * cap, home_score.shape[2])
            logits = logit_ref[...]
            lanes = lax.broadcasted_iota(jnp.int32, logits.shape, 1)
            scores = [
                jnp.dot(
                    one_hot(k).astype(F32), arrived,
                    precision=lax.Precision.HIGHEST, preferred_element_type=F32,
                )
                for k in range(top)
            ]
            probs = [small_ref[:, k:k + 1] for k in range(top)]
            mean = sum(p * q for p, q in zip(probs, scores))
            z_weight = small_ref[:, top + 1:top + 2]
            log_total = small_ref[:, top:top + 1]
            grad = 2.0 * z_weight * log_total * jnp.exp(logits - log_total)
            for k in range(top):
                grad = grad + jnp.where(
                    spot_ref[:, top + k:top + k + 1] == lanes, probs[k] * (scores[k] - mean), 0.0
                )
            lg_ref[...] = grad.astype(BF16)
            rp_ref[...] = jnp.dot(tok_ref[...].T, lg_ref[...], preferred_element_type=F32)
            for k in range(1, flight):
                share_e(k).start()

        @pl.when(step == 2)
        def _():
            total = rp_ref[pl.ds(pl.multiple_of(e * piece_e, piece_e), piece_e), :]
            for k in range(1, flight):
                share_e(k).wait_recv()
                total = total + rx_e[k - 1]
            rp_ref[pl.ds(pl.multiple_of(e * piece_e, piece_e), piece_e), :] = total
            rsum[...] = total.astype(BF16)
            for k in range(1, n):
                share_d(k).start()

        @pl.when(step == 3)
        def _():
            mine = pl.ds(pl.multiple_of(e * piece_e + d * piece_d, piece_d), piece_d)
            total = rp_ref[mine, :]
            for k in range(1, n):
                share_d(k).wait_recv()
                total = total + rx_d[k - 1].astype(F32)
            rfull[mine, :] = total
            for k in range(1, n):
                gather_d(k, d).start()

        @pl.when(step == 4)
        def _():
            for k in range(1, n):
                gather_d(k, lax.rem(d + n - k, n)).wait_recv()
            for k in range(1, flight):
                gather_e(k, e).start()

        @pl.when(step == 5)
        def _():
            for k in range(1, flight):
                give_dx(k, from_peer(k)).wait_recv()
            picks = sum(one_hot(k).astype(F32) for k in range(top)).astype(BF16)
            rows = home_dx[...]
            for col in range(0, width, tile):
                total = jnp.dot(picks, rows[:, col:col + tile], preferred_element_type=F32)
                total = total + lax.dot_general(
                    lg_ref[...], rw_ref[col:col + tile, :], (((1,), (1,)), ((), ())),
                    preferred_element_type=F32,
                )
                tg_ref[:, col:col + tile] = total.astype(BF16)

        return carry

    lax.fori_loop(1, n - 1, middle, 0)

    for k in range(1, flight):
        gather_e(k, from_peer(k)).wait_recv()
    rout_ref[...] = rfull[...]
    for part in range(3):
        for way in range(2):
            hop(way, part, n - 2).wait_recv()
            total = slot(way, part, n - 1)[...].astype(F32) + own(way, part, d)
            if part < 2:
                gu_ref[
                    0, part * half_rows:(part + 1) * half_rows, way * gu_cols:(way + 1) * gu_cols
                ] = total.astype(BF16)
            else:
                dn_ref[0, :, way * dn_cols:(way + 1) * dn_cols] = total.astype(BF16)

    def drain(step, carry):
        for part in range(3):
            for way in range(2):
                hop(way, part, step).wait_send()
        return carry

    lax.fori_loop(0, n - 1, drain, 0)
    for k in range(1, n):
        share_d(k).wait_send()
        gather_d(k, d).wait_send()
    for k in range(1, flight):
        share_e(k).wait_send()
        gather_e(k, e).wait_send()
        give_score(k, e).wait_send()
        give_dx(k, e).wait_send()


def rows_part(
    flight, cap,
    tok_ref, og_ref, rw_ref, ids_ref, zw_ref, load_g, load_d, greet,
    xt_ref, ht_ref, pg_ref, score_ref, logit_ref, small_ref, spot_ref,
    wg_ref, wd_ref, out_x, out_o, out_p, in_x, in_o, in_p, pre, hid,
    x_send, x_recv, o_send, o_recv, p_send, p_recv,
):
    d = lax.axis_index("dp")
    e = lax.axis_index("expert")
    top, tok_count = ids_ref.shape
    routed = rw_ref.shape[1]
    hidden_units, width = wd_ref.shape
    tile = min(hidden_units, 512)
    pairs = flight // 2
    lanes = lax.broadcasted_iota(jnp.int32, (tok_count, routed), 1)
    def column(row):
        return jnp.broadcast_to(row, (routed, tok_count)).T

    ids = [column(ids_ref[k:k + 1, :].astype(F32)).astype(jnp.int32) for k in range(top)]
    choose = [column_ids == lanes for column_ids in ids]
    member = sum(c.astype(F32) for c in choose)
    earlier = lax.broadcasted_iota(jnp.int32, (tok_count, tok_count), 0) > (
        lax.broadcasted_iota(jnp.int32, (tok_count, tok_count), 1)
    )
    rank = jnp.dot(earlier.astype(F32).astype(BF16), member.astype(BF16), preferred_element_type=F32)
    rank = jnp.where(member > 0.0, rank, -1.0)
    by_expert = rank.T.astype(jnp.int32)
    ranks = lax.broadcasted_iota(jnp.int32, (cap, tok_count), 0)
    picks = [by_expert[f:f + 1, :] == ranks for f in range(flight)]

    greet()

    def rows_of(index):
        return pl.ds(pl.multiple_of(index * cap, cap), cap)

    def peers():
        found = []
        for i in range(1, pairs):
            pair = lax.rem(lax.div(e, 2) + i, pairs)
            found += [pair * 2 + lax.rem(e, 2), pair * 2 + 1 - lax.rem(e, 2)]
        return found + [lax.div(e, 2) * 2 + 1 - lax.rem(e, 2)]

    def give(out, into, sends, recvs, source, target):
        return pltpu.make_async_remote_copy(
            src_ref=out.at[rows_of(target), :], dst_ref=into.at[rows_of(source), :],
            send_sem=sends.at[target], recv_sem=recvs.at[source],
            device_id=(d, target), device_id_type=MESH,
        )

    give_x = functools.partial(give, out_x, in_x, x_send, x_recv)
    give_o = functools.partial(give, out_o, in_o, o_send, o_recv)
    give_p = functools.partial(give, out_p, in_p, p_send, p_recv)

    for f in range(flight):
        out_x[f * cap:(f + 1) * cap, :] = jnp.dot(
            picks[f].astype(F32).astype(BF16), tok_ref[...], preferred_element_type=F32
        ).astype(BF16)
    for to in peers():
        give_x(e, to).start()
    for f in range(flight):
        out_o[f * cap:(f + 1) * cap, :] = jnp.dot(
            picks[f].astype(F32).astype(BF16), og_ref[...], preferred_element_type=F32
        ).astype(BF16)
    for to in peers():
        give_o(e, to).start()

    logits = jnp.dot(tok_ref[...], rw_ref[...], preferred_element_type=F32)
    logit_ref[...] = logits
    chosen = [
        jnp.exp(jnp.sum(jnp.where(c, logits, 0.0), axis=1, keepdims=True)) for c in choose
    ]
    norm = sum(chosen)
    probs = [c / norm for c in chosen]
    log_total = jnp.log(jnp.sum(jnp.exp(logits), axis=1, keepdims=True))
    small = jnp.where(lanes == top, log_total, column(zw_ref[...]))
    spot = jnp.full(lanes.shape, -1, jnp.int32)
    weight = jnp.zeros(lanes.shape, F32)
    place = jnp.where((rank >= 0.0) & (lanes < flight), rank + (lanes * cap).astype(F32) + 1.0, 0.0)
    for k in range(top):
        small = jnp.where(lanes == k, probs[k], small)
        at = jnp.sum(jnp.where(choose[k], place, 0.0), axis=1, keepdims=True) - 1.0
        spot = jnp.where(lanes == k, at.astype(jnp.int32), spot)
        spot = jnp.where(lanes == top + k, ids[k], spot)
        weight = weight + jnp.where(choose[k], probs[k], 0.0)
    small_ref[...] = small
    spot_ref[...] = spot
    weight = weight.T
    for f in range(flight):
        row = jnp.sum(jnp.where(picks[f], weight[f:f + 1, :], 0.0), axis=1, keepdims=True)
        out_p[f * cap:(f + 1) * cap, :] = jnp.broadcast_to(row, (cap, routed))
    for to in peers():
        give_p(e, to).start()
    in_x[rows_of(e), :] = out_x[rows_of(e), :]
    in_o[rows_of(e), :] = out_o[rows_of(e), :]
    in_p[rows_of(e), :] = out_p[rows_of(e), :]

    def arrived(gives, pair):
        for core in range(2):
            source = pair * 2 + core

            @pl.when(source != e)
            def _():
                for g in gives:
                    g(source, e).wait_recv()

    def pair_rows(pair):
        return pl.ds(pl.multiple_of(pair * (2 * cap), 2 * cap), 2 * cap)

    load_g.wait()
    load_d.wait()

    def one_pair(i, carry):
        pair = lax.rem(lax.div(e, 2) + i, pairs)
        rows = pair_rows(pair)
        arrived([give_x], pair)
        for col in range(0, 2 * hidden_units, tile):
            pre[:, col:col + tile] = jnp.dot(
                in_x[rows, :], wg_ref[:, col:col + tile], preferred_element_type=F32
            )
        xt_ref[:, rows] = in_x[rows, :].T
        arrived([give_o, give_p], pair)
        prob = in_p[rows, 0:1]
        score = jnp.zeros((2 * cap, 1), F32)
        for col in range(0, hidden_units, tile):
            raw = lax.dot_general(
                in_o[rows, :], wd_ref[col:col + tile, :], (((1,), (1,)), ((), ())),
                preferred_element_type=F32,
            )
            gate = pre[:, col:col + tile]
            up = pre[:, hidden_units + col:hidden_units + col + tile]
            sig = jax.nn.sigmoid(gate)
            active = gate * sig
            hidden = (active * up).astype(BF16)
            hid[:, col:col + tile] = hidden
            score = score + jnp.sum(raw * hidden.astype(F32), axis=1, keepdims=True)
            grad = prob * raw
            pg_ref[rows, col:col + tile] = (
                grad * up * sig * (1.0 + gate * (1.0 - sig))
            ).astype(BF16)
            pg_ref[rows, hidden_units + col:hidden_units + col + tile] = (grad * active).astype(BF16)
        score_ref[rows, :] = jnp.broadcast_to(score, (2 * cap, routed))
        in_o[rows, :] = (prob * in_o[rows, :].astype(F32)).astype(BF16)
        ht_ref[:, rows] = hid[...].T
        return carry

    lax.fori_loop(0, pairs, one_pair, 0)
    for to in peers():
        give_x(e, to).wait_send()
        give_o(e, to).wait_send()
        give_p(e, to).wait_send()


def layer_kernel(copies, flight, order, cap, *refs):
    tok_ref, og_ref, rw_ref, ids_ref, zw_ref, wg_hbm, wd_hbm = refs[:7]
    outs = refs[7:11]
    xt, ht, pg, score, logit, small, spot, wg_ref, wd_ref = refs[11:20]
    rows_scratch = refs[20:28]
    wg_sem, wd_sem = refs[28:30]
    rows_sems = refs[30:36]
    grads_scratch = refs[36:]
    out_x, in_x, dy = rows_scratch[0], rows_scratch[3], rows_scratch[4]
    d = lax.axis_index("dp")
    e = lax.axis_index("expert")
    load_g = pltpu.make_async_copy(wg_hbm, wg_ref, wg_sem)
    load_d = pltpu.make_async_copy(wd_hbm, wd_ref, wd_sem)
    load_g.start()
    load_d.start()
    barrier = pltpu.get_barrier_semaphore()
    for k in range(1, flight):
        to = lax.rem(e + k, flight)
        pl.semaphore_signal(barrier, inc=1, device_id=(d, to), device_id_type=MESH)
    for k in range(1, copies):
        to = lax.rem(d + k, copies)
        pl.semaphore_signal(barrier, inc=1, device_id=(to, e), device_id_type=MESH)

    def greet():
        pl.semaphore_wait(barrier, copies + flight - 2)

    rows_part(
        flight, cap, tok_ref, og_ref, rw_ref, ids_ref, zw_ref, load_g, load_d, greet,
        xt, ht, pg, score, logit, small, spot, wg_ref, wd_ref, *rows_scratch, *rows_sems,
    )
    grads_part(
        copies, flight, order, ids_ref.shape[0],
        tok_ref, rw_ref, wg_ref, xt, pg, ht, dy, score, logit, small, spot, out_x, in_x,
        *outs, *grads_scratch,
    )


def finish_kernel(*refs):
    for source, target in zip(refs[:4], refs[4:]):
        target[...] = source[...]


def per_device(tokens, out_grad, z_weight, router_weight, expert_ids, gate_up_weight, down_weight):
    n = lax.axis_size("dp")
    flight = lax.axis_size("expert")
    w_gateup, w_down = gate_up_weight[0], down_weight[0]
    tok_count, width = tokens.shape
    routed = router_weight.shape[1]
    hidden = w_down.shape[0]
    gate_up = w_gateup.shape[1]
    cap = tok_count // 2
    rows = flight * cap
    gu_rows, dn_rows = width // n, hidden // n
    piece_e = width // flight
    piece_d = piece_e // n
    dma = pltpu.SemaphoreType.DMA
    vmem = pl.BlockSpec(memory_space=pltpu.VMEM)
    hbm = pl.BlockSpec(memory_space=pl.ANY)
    shape = jax.ShapeDtypeStruct
    gate_up_grad, down_grad, router_grad, token_grad = pl.pallas_call(
        functools.partial(layer_kernel, n, flight, ring_order(n), cap),
        out_shape=(
            shape((1, gu_rows, gate_up), BF16),
            shape((1, dn_rows, width), BF16),
            shape((width, routed), F32),
            shape((tok_count, width), BF16),
        ),
        in_specs=[vmem] * 5 + [hbm] * 2,
        out_specs=(vmem,) * 4,
        scratch_shapes=[
            pltpu.VMEM((width, rows), BF16),
            pltpu.VMEM((hidden, rows), BF16),
            pltpu.VMEM((rows, gate_up), BF16),
            pltpu.VMEM((rows, routed), F32),
            pltpu.VMEM((tok_count, routed), F32),
            pltpu.VMEM((tok_count, routed), F32),
            pltpu.VMEM((tok_count, routed), jnp.int32),
            pltpu.VMEM(w_gateup.shape, BF16),
            pltpu.VMEM(w_down.shape, BF16),
            pltpu.VMEM((rows, width), BF16),
            pltpu.VMEM((rows, width), BF16),
            pltpu.VMEM((rows, routed), F32),
            pltpu.VMEM((rows, width), BF16),
            pltpu.VMEM((rows, width), BF16),
            pltpu.VMEM((rows, routed), F32),
            pltpu.VMEM((2 * cap, gate_up), F32),
            pltpu.VMEM((2 * cap, hidden), BF16),
            dma, dma,
        ] + [dma((flight,))] * 6 + [
            pltpu.VMEM((2, 2, n, gu_rows // 2, gate_up // 2), BF16),
            pltpu.VMEM((2, n, dn_rows, width // 2), BF16),
            pltpu.VMEM((flight - 1, piece_e, routed), F32),
            pltpu.VMEM((piece_e, routed), BF16),
            pltpu.VMEM((n - 1, piece_d, routed), BF16),
            pltpu.VMEM((width, routed), F32),
            pltpu.VMEM((width, routed), F32),
            pltpu.VMEM((flight, cap, routed), F32),
            pltpu.VMEM((tok_count, routed), BF16),
            dma((2, 3, n - 1)), dma((2, 3, n - 1)),
            dma((flight - 1,)), dma((flight - 1,)),
            dma((n - 1,)), dma((n - 1,)),
            dma((n - 1,)), dma((n - 1,)),
            dma((flight - 1,)), dma((flight - 1,)),
            dma((flight - 1,)), dma((flight - 1,)),
            dma((flight - 1,)), dma((flight - 1,)),
        ],
        compiler_params=pltpu.CompilerParams(
            collective_id=0, has_side_effects=True, vmem_limit_bytes=67_000_000
        ),
        name="layer",
    )(
        tokens,
        out_grad,
        router_weight,
        expert_ids.T,
        z_weight[None, :],
        w_gateup,
        w_down,
    )
    results = (token_grad, router_grad, gate_up_grad, down_grad)
    return pl.pallas_call(
        finish_kernel,
        out_shape=tuple(shape(r.shape, r.dtype) for r in results),
        in_specs=[vmem] * 4,
        out_specs=(vmem,) * 4,
        compiler_params=pltpu.CompilerParams(vmem_limit_bytes=16 * 2**20),
        name="finish",
    )(*results)


def solution(mesh):
    return jax.shard_map(
        per_device,
        mesh=mesh,
        in_specs=(
            P(("dp", "expert"), None),
            P(("dp", "expert"), None),
            P(("dp", "expert")),
            P(),
            P(("dp", "expert"), None),
            P("expert", None, None),
            P("expert", None, None),
        ),
        out_specs=(
            P(("dp", "expert"), None),
            P(),
            P("expert", "dp", None),
            P("expert", "dp", None),
        ),
        check_vma=False,
    )
```

profile of v0, /device:TPU:0, one launch (start us, length us, event | category | flops | bytes accessed | tf_op | source)
XLA Modules:
  0.0 232.5 jit_solution(11917615010227782740)
XLA Ops:
  0.6 224.9 %layer.1 = (bf16[1,256,3072]{2,1,0:T(8,128)(2,1)}, bf16[1,192,2048]{2,1,0:T(8,128)(2,1)}, f32[2048,128]{1,0:T(8,128)}, bf16[128,2048]{1,0:T(8,128)(2,1)}) custom-call(bf16[128,2048]{1,0:T(8,128)(2,1)} %refs_0_.1, bf16[128,2048]{1,0:T(8,128)(2,1)} %refs_1_.1, bf16[2048,128]{1,0:T(8,128)(2,1)} %refs_2_.1, s32[4,128]{1,0:T(4,128)} %bitcast.6, ...), custom_call_target="tpu_custom_call" | custom-call | tf_op jit(solution)/shard_map/layer/pallas_call | solution.py:501
  225.5 0.0 copy-start
  225.6 1.4 copy-done
  227.0 0.0 copy-start.1
  227.0 1.2 copy-done.1
  228.2 0.0 copy-start.2
  228.2 1.1 copy-done.2
  229.3 0.0 copy-start.3
  229.3 1.0 copy-done.3
  230.4 2.2 finish.1
Async XLA Ops:
  225.5 1.4 copy-start
  227.0 1.2 copy-start.1
  228.2 1.1 copy-start.2
  229.3 1.0 copy-start.3
where the time goes:
time: 233 us
  Pallas kernels  227 us (97%)
  local copies, waits for them, and re-layouts  4.8 us (2%)
    pallas_call x1, Pallas kernels, per_device(): pl.pallas_call(functools.partial(layer_kernel, n, flight, ring_order(n),...  225 us
    unnamed x8, local copies, waits for them, and re-layouts  4.8 us

commit v1 on v0

v1 whole, which is shorter than its diff:
```python
import functools
import heapq
import itertools
import math

import jax
import jax.numpy as jnp
from jax import lax
from jax.experimental import pallas as pl
from jax.experimental.pallas import tpu as pltpu
from jax.sharding import PartitionSpec as P

F32 = jnp.float32
BF16 = jnp.bfloat16
MESH = pl.DeviceIdType.MESH
TOKENS, COTANGENTS, META, LOGIT = range(4)
LINK_RATE = 46.6e3
LINK_DELAY = 3.0


def lookup(table, key):
    value = jnp.int32(0)
    for slot, entry in enumerate(table):
        if entry:
            value = value + jnp.where(key == slot, jnp.int32(entry), jnp.int32(0))
    return value


def grid_of(copies, flight):
    inner = max(k for k in range(1, copies + 1) if copies % k == 0 and k * k <= copies)
    return dict(z=copies // inner, x=inner, y=flight // 2)


def visit_order(size):
    return [
        [i] + sorted((k for k in range(size) if k != i), key=lambda k: (abs(k - i), k < i))
        for i in range(size)
    ]


def make_parts(grid, tok_count):
    straight, crossed = ("x", "z", "y"), ("y", "z", "x")
    first_x, first_y = ("z", "x", "y"), ("z", "y", "x")
    if math.prod(grid.values()) > 16 or tok_count % 128:
        pieces = [(0, tok_count, straight, crossed)]
    else:
        unit = tok_count // 8
        pieces = [
            (0, 3 * unit, first_x, first_y),
            (3 * unit, 3 * unit, straight, crossed),
            (6 * unit, 2 * unit, straight, crossed),
        ]
    parts = []
    for start, rows, order_x, order_o in pieces:
        parts += [(TOKENS, start, rows, order_x), (COTANGENTS, start, rows, order_o)]
    return parts + [(META, 0, 0, first_x), (LOGIT, 0, 0, first_x)]


def routes(grid, order, source, here):
    last = max((i for i, d in enumerate(order) if source[d] != here[d]), default=-1)
    found = []
    if last >= 0:
        d = order[last]
        way = 1 if source[d] < here[d] else -1
        if 0 <= here[d] + way < grid[d]:
            found.append((d, way))
    for d in order[last + 1:]:
        for way in (1, -1):
            if 0 <= here[d] + way < grid[d]:
                found.append((d, way))
    return found


def mean_arrivals(grid, parts, sizes, starts):
    dims = list(grid)
    visits = {d: visit_order(grid[d]) for d in dims}
    nodes = [dict(zip(dims, at)) for at in itertools.product(*[range(grid[d]) for d in dims])]
    queue, free, count, times = [], {}, itertools.count(), {}

    def spread(time, here, part, source):
        for d, way in routes(grid, parts[part][3], source, here):
            key = (tuple(here.values()), d, way)
            begin = max(time, free.get(key, 0.0))
            free[key] = begin + sizes[part] / LINK_RATE
            there = dict(here)
            there[d] += way
            heapq.heappush(queue, (free[key] + LINK_DELAY, next(count), there, part, source))

    for part in range(len(parts)):
        for here in nodes:
            heapq.heappush(queue, (starts[part], next(count), here, part, here))
    while queue:
        time, _, here, part, source = heapq.heappop(queue)
        if source != here:
            key = (part, tuple(visits[d][here[d]].index(source[d]) for d in dims))
            times.setdefault(key, []).append(time)
        spread(time, here, part, source)
    return {key: sum(found) / len(found) for key, found in times.items()}


def make_plan(grid, parts, sizes, starts, chunk_times, send_slot):
    arrivals = sorted((time, key) for key, time in mean_arrivals(grid, parts, sizes, starts).items())
    groups, chunks = len(chunk_times), len(chunk_times[0])
    last = {}
    for index, (_, (part, (jz, jx, jy))) in enumerate(arrivals):
        if parts[part][0] != LOGIT:
            last[jz * grid["x"] + jx] = index
    router_from = groups // 2
    for index, (_, (part, (jz, jx, jy))) in enumerate(arrivals):
        if parts[part][0] == LOGIT:
            user = router_from + (jz * grid["x"] + jx) // 2
            last[user] = max(last.get(user, -1), index)
    slots = [[[] for _ in range(chunks)] for _ in range(groups)]
    late, now, done, held = [], 0.0, 0, []
    for group in range(groups):
        for chunk in range(chunks):
            here = slots[group][chunk]
            sent = (group, chunk) > send_slot
            if sent and held:
                here += held
                held = []
            while done < len(arrivals) and (arrivals[done][0] <= now or done <= last.get(group, -1)):
                time, key = arrivals[done]
                if parts[key[0]][0] == LOGIT and not sent:
                    held.append(key)
                else:
                    here.append(key)
                now = max(now, time)
                done += 1
            now += chunk_times[group][chunk]
    late = held + [key for _, key in arrivals[done:]]
    return slots, late


class Sites:
    def __init__(self, grid, parts):
        self.index = {}
        visits = [range(grid[d]) for d in grid]
        dims = list(grid)
        for part, (_, _, _, order) in enumerate(parts):
            for js in itertools.product(*visits):
                at = dict(zip(dims, js))
                last = max((i for i, d in enumerate(order) if at[d]), default=-1)
                kinds = []
                if last >= 0 and grid[order[last]] > 2:
                    kinds.append((order[last], 0))
                for d in order[last + 1:]:
                    if grid[d] == 2:
                        kinds.append((d, 0))
                    elif grid[d] > 2:
                        kinds += [(d, 1), (d, -1)]
                kinds.append(("core", 0))
                for kind in kinds:
                    self.index[(part, js, kind)] = len(self.index)

    def of(self, part, js):
        return [key[2] for key in self.index if key[0] == part and key[1] == js]


def layer_kernel(copies, flight, cap, grid, parts, sites, slots, late, send_slot, *refs):
    (tok_ref, og_ref, rw_ref, ids_ref, zw_ref, wg_hbm, wd_hbm,
     gu_ref, dn_ref, rout_ref, tg_ref, gx, go,
     wg_ref, wd_ref, xb, ob, rows_x, rows_o, prob_ref, pg_ref, hid, acc_gu, acc_dn,
     logit_ref, small_ref, spot_ref, mref, lref, rgt, back, home_dx, score_ref, home_score,
     wg_sem, wd_sem, own_sem, load_sem, send_sem, recv_sem,
     sc_send, sc_recv, dx_send, dx_recv) = refs
    d = lax.axis_index("dp")
    e = lax.axis_index("expert")
    dims = list(grid)
    top, tok_count = ids_ref.shape
    routed = rw_ref.shape[1]
    hidden_units, width = wd_ref.shape
    rows_group = flight * tok_count
    tile = min(hidden_units, 512)
    wide = min(width, 512)
    gu_rows, dn_rows = gu_ref.shape[1], dn_ref.shape[1]
    core = lax.rem(e, 2)
    my = dict(z=lax.div(d, grid["x"]), x=lax.rem(d, grid["x"]), y=lax.div(e, 2))
    visits = {k: visit_order(grid[k]) for k in dims}
    coord = {
        k: [lookup([visits[k][p][j] for p in range(grid[k])], my[k]) for j in range(grid[k])]
        for k in dims
    }

    def place(at, which):
        return (at["z"] * grid["x"] + at["x"], at["y"] * 2 + which)

    def block_index(at, which):
        dp, expert = place(at, which)
        return dp * flight + expert

    me = block_index(my, core)

    def slice_of(part, index, own=False):
        kind, start, rows, _ = parts[part]
        if kind == META:
            return mref.at[index]
        if kind == LOGIT:
            return lref.at[pl.ds(pl.multiple_of(index * tok_count, tok_count), tok_count), :]
        if own:
            return (tok_ref if kind == TOKENS else og_ref).at[pl.ds(start, rows), :]
        unit = math.gcd(start, tok_count) if start else tok_count
        return (gx if kind == TOKENS else go).at[
            pl.ds(pl.multiple_of(index * tok_count + start, unit), rows), :
        ]

    def arrival(part, index):
        there = slice_of(part, index)
        return pltpu.make_async_remote_copy(
            src_ref=there, dst_ref=there, send_sem=send_sem.at[0],
            recv_sem=recv_sem.at[part, index], device_id=(d, e), device_id_type=MESH,
        )

    def outgoing(part, js, kind):
        at = {k: coord[k][j] for k, j in zip(dims, js)}
        dim, way = kind
        target, guard, which = dict(my), None, core
        if dim == "core":
            which = 1 - core
        elif way == 0 and not at[dim] is my[dim] and js[dims.index(dim)]:
            ahead = my[dim] + jnp.where(at[dim] < my[dim], 1, -1)
            guard = (ahead >= 0) & (ahead < grid[dim])
            target[dim] = ahead
        elif way == 0:
            target[dim] = 1 - my[dim]
        else:
            ahead = my[dim] + way
            guard = (ahead < grid[dim]) if way > 0 else (ahead >= 0)
            target[dim] = ahead
        index = block_index(at, core)
        site = sites.index[(part, js, kind)]
        copy = pltpu.make_async_remote_copy(
            src_ref=slice_of(part, index, own=not any(js)), dst_ref=slice_of(part, index),
            send_sem=send_sem.at[site], recv_sem=recv_sem.at[part, index],
            device_id=place(target, which), device_id_type=MESH,
        )
        return guard, copy

    def each(part, js, act):
        for kind in sites.of(part, js):
            guard, copy = outgoing(part, js, kind)
            if guard is None:
                act(copy)
            else:
                pl.when(guard)(functools.partial(act, copy))

    def handle(event):
        part, js = event
        at = {k: coord[k][j] for k, j in zip(dims, js)}
        arrival(part, block_index(at, core)).wait_recv()
        each(part, js, lambda copy: copy.start())

    home = (0,) * len(dims)

    def start_own(kinds):
        for part, (kind, *_) in enumerate(parts):
            if kind in kinds:
                each(part, home, lambda copy: copy.start())

    barrier = pltpu.get_barrier_semaphore()
    for k in range(1, flight):
        pl.semaphore_signal(
            barrier, inc=1, device_id=(d, lax.rem(e + k, flight)), device_id_type=MESH
        )
    greeted = jnp.int32(flight - 1)
    for k in ("z", "x"):
        for way in (1, -1):
            ahead = my[k] + way
            there = (ahead < grid[k]) if way > 0 else (ahead >= 0)
            greeted = greeted + jnp.where(there, 1, 0)

            @pl.when(there)
            def _():
                target = dict(my)
                target[k] = ahead
                pl.semaphore_signal(
                    barrier, inc=1, device_id=place(target, core), device_id_type=MESH
                )

    load_g = pltpu.make_async_copy(wg_hbm, wg_ref, wg_sem)
    load_d = pltpu.make_async_copy(wd_hbm, wd_ref, wd_sem)
    load_g.start()
    load_d.start()
    mine = pl.ds(pl.multiple_of(me * tok_count, tok_count), tok_count)
    own_x = pltpu.make_async_copy(tok_ref, gx.at[mine, :], own_sem.at[0])
    own_o = pltpu.make_async_copy(og_ref, go.at[mine, :], own_sem.at[1])
    own_x.start()
    own_o.start()
    pl.semaphore_wait(barrier, greeted)
    start_own((TOKENS, COTANGENTS))

    lanes = lax.broadcasted_iota(jnp.int32, (tok_count, routed), 1)

    def column(row):
        return jnp.broadcast_to(row, (routed, tok_count)).T

    ids = [column(ids_ref[k:k + 1, :].astype(F32)).astype(jnp.int32) for k in range(top)]
    choose = [column_ids == lanes for column_ids in ids]
    member = sum(c.astype(F32) for c in choose)
    earlier = lax.broadcasted_iota(jnp.int32, (tok_count, tok_count), 0) > (
        lax.broadcasted_iota(jnp.int32, (tok_count, tok_count), 1)
    )
    rank = jnp.dot(earlier.astype(F32).astype(BF16), member.astype(BF16), preferred_element_type=F32)
    rank = jnp.where(member > 0.0, rank, -1.0)
    logits = jnp.dot(tok_ref[...], rw_ref[...], preferred_element_type=F32)
    chosen = [
        jnp.exp(jnp.sum(jnp.where(c, logits, 0.0), axis=1, keepdims=True)) for c in choose
    ]
    norm = sum(chosen)
    probs = [c / norm for c in chosen]
    weight = jnp.zeros(lanes.shape, F32)
    for k in range(top):
        weight = weight + jnp.where(choose[k], probs[k], 0.0)
    mref[me, 0:flight, :] = rank.T[0:flight, :]
    mref[me, flight:2 * flight, :] = weight.T[0:flight, :]
    start_own((META,))
    logit_ref[...] = logits
    log_total = jnp.log(jnp.sum(jnp.exp(logits), axis=1, keepdims=True))
    small = jnp.where(lanes == top, log_total, column(zw_ref[...]))
    spot = jnp.full(lanes.shape, -1, jnp.int32)
    spots = jnp.where((rank >= 0.0) & (lanes < flight), rank + (lanes * cap).astype(F32) + 1.0, 0.0)
    for k in range(top):
        small = jnp.where(lanes == k, probs[k], small)
        at = jnp.sum(jnp.where(choose[k], spots, 0.0), axis=1, keepdims=True) - 1.0
        spot = jnp.where(lanes == k, at.astype(jnp.int32), spot)
        spot = jnp.where(lanes == top + k, ids[k], spot)
    small_ref[...] = small
    spot_ref[...] = spot
    acc_gu[...] = jnp.zeros_like(acc_gu)
    acc_dn[...] = jnp.zeros_like(acc_dn)
    rgt[...] = jnp.zeros_like(rgt)

    window = acc_dn.shape[0]
    dn_unit = math.gcd(dn_rows, 128)
    dn_start = jnp.minimum(lax.div(d * dn_rows, 128) * 128, hidden_units - window)
    dn_off = pl.multiple_of(d * dn_rows - dn_start, dn_unit)
    dn_start = pl.multiple_of(dn_start, 128)

    def group_at(j):
        jz, jx = lax.div(j, grid["x"]), lax.rem(j, grid["x"])
        z = lookup(sum(visits["z"], []), my["z"] * grid["z"] + jz)
        x = lookup(sum(visits["x"], []), my["x"] * grid["x"] + jx)
        return z * grid["x"] + x

    def wait_sibling(group, kinds):
        for y in range(grid["y"]):
            index = group * flight + 2 * y + 1 - core
            for part, (kind, *_) in enumerate(parts):
                if kind in kinds:
                    arrival(part, index).wait_recv()

    def load_x(group):
        rows = pl.ds(pl.multiple_of(group * rows_group, rows_group), rows_group)
        return pltpu.make_async_copy(gx.at[rows, :], xb, load_sem.at[0])

    def load_o(group):
        rows = pl.ds(pl.multiple_of(group * rows_group, rows_group), rows_group)
        return pltpu.make_async_copy(go.at[rows, :], ob, load_sem.at[1])

    ranks = lax.broadcasted_iota(jnp.int32, (cap, tok_count), 0).astype(F32)

    def gather_rows(group):
        wait_sibling(group, (TOKENS, COTANGENTS, META))
        load_x(group).start()
        load_o(group).start()
        picks = []
        for s in range(flight):
            index = group * flight + s
            pick = mref[index, pl.ds(e, 1), :] == ranks
            part = jnp.where(pick, mref[index, pl.ds(flight + e, 1), :], 0.0)
            prob = jnp.sum(part, axis=1, keepdims=True)
            prob_ref[s * cap:(s + 1) * cap, :] = jnp.broadcast_to(prob, (cap, prob_ref.shape[1]))
            picks.append(pick.astype(F32).astype(BF16))
        load_x(group).wait()
        load_o(group).wait()
        for s in range(flight):
            rows = slice(s * cap, (s + 1) * cap)
            toks = slice(s * tok_count, (s + 1) * tok_count)
            rows_x[rows, :] = jnp.dot(
                picks[s], xb[toks, :], preferred_element_type=F32
            ).astype(BF16)
            rows_o[rows, :] = jnp.dot(
                picks[s], ob[toks, :], preferred_element_type=F32
            ).astype(BF16)

    def hidden_tile(col, own):
        gate = jnp.dot(rows_x[...], wg_ref[:, col:col + tile], preferred_element_type=F32)
        up = jnp.dot(
            rows_x[...], wg_ref[:, hidden_units + col:hidden_units + col + tile],
            preferred_element_type=F32,
        )
        raw = lax.dot_general(
            rows_o[...], wd_ref[col:col + tile, :], (((1,), (1,)), ((), ())),
            preferred_element_type=F32,
        )
        sig = jax.nn.sigmoid(gate)
        active = gate * sig
        hidden = (active * up).astype(BF16)
        hid[:, col:col + tile] = hidden
        grad = prob_ref[:, 0:1] * raw
        pg_ref[:, col:col + tile] = (grad * up * sig * (1.0 + gate * (1.0 - sig))).astype(BF16)
        pg_ref[:, hidden_units + col:hidden_units + col + tile] = (grad * active).astype(BF16)

        @pl.when(own)
        def _():
            part = jnp.sum(raw * hidden.astype(F32), axis=1, keepdims=True)
            part = jnp.broadcast_to(part, score_ref.shape)
            score_ref[...] = part if col == 0 else score_ref[...] + part

    def weight_grads():
        rows_o[...] = (prob_ref[:, 0:1] * rows_o[...].astype(F32)).astype(BF16)
        taken = rows_x[:, pl.ds(pl.multiple_of(d * gu_rows, gu_rows), gu_rows)]
        for col in range(0, 2 * hidden_units, tile):
            acc_gu[:, col:col + tile] += lax.dot_general(
                taken, pg_ref[:, col:col + tile], (((0,), (0,)), ((), ())),
                preferred_element_type=F32,
            )
        taken = hid[:, pl.ds(dn_start, window)]
        for col in range(0, width, wide):
            acc_dn[:, col:col + wide] += lax.dot_general(
                taken, rows_o[:, col:col + wide], (((0,), (0,)), ((), ())),
                preferred_element_type=F32,
            )

    def block(ref, index):
        return ref.at[pl.ds(pl.multiple_of(index * cap, cap), cap), :]

    def give_score(k, source):
        to = lax.rem(e + k, flight)
        return pltpu.make_async_remote_copy(
            src_ref=block(score_ref, to), dst_ref=home_score.at[source],
            send_sem=sc_send.at[k - 1], recv_sem=sc_recv.at[k - 1],
            device_id=(d, to), device_id_type=MESH,
        )

    def give_dx(k, source):
        to = lax.rem(e + k, flight)
        return pltpu.make_async_remote_copy(
            src_ref=block(back, to), dst_ref=block(home_dx, source),
            send_sem=dx_send.at[k - 1], recv_sem=dx_recv.at[k - 1],
            device_id=(d, to), device_id_type=MESH,
        )

    def from_peer(k):
        return lax.rem(e + flight - k, flight)

    def one_hot(k):
        across = lax.broadcasted_iota(jnp.int32, (tok_count, flight * cap), 1)
        return across == spot_ref[:, k:k + 1]

    def row_grads(first, last):
        for col in range(first, last, wide):
            back[:, col:col + wide] = lax.dot_general(
                pg_ref[...], wg_ref[col:col + wide, :], (((1,), (1,)), ((), ())),
                preferred_element_type=F32,
            ).astype(BF16)

    half = width // 2 // wide * wide

    def send_scores():
        for k in range(1, flight):
            give_score(k, e).start()
        home_score[e] = score_ref[pl.ds(pl.multiple_of(e * cap, cap), cap), :]
        row_grads(0, half)

    def send_rows():
        row_grads(half, width)
        for k in range(1, flight):
            give_dx(k, e).start()
        own_rows = pl.ds(pl.multiple_of(e * cap, cap), cap)
        home_dx[own_rows, :] = back[own_rows, :]

    def logit_grads():
        for k in range(1, flight):
            give_score(k, from_peer(k)).wait_recv()
        arrived = home_score[...].reshape(flight * cap, home_score.shape[2])
        logits = logit_ref[...]
        scores = [
            jnp.dot(
                one_hot(k).astype(F32), arrived,
                precision=lax.Precision.HIGHEST, preferred_element_type=F32,
            )
            for k in range(top)
        ]
        probs = [small_ref[:, k:k + 1] for k in range(top)]
        mean = sum(p * q for p, q in zip(probs, scores))
        z_weight = small_ref[:, top + 1:top + 2]
        log_total = small_ref[:, top:top + 1]
        grad = 2.0 * z_weight * log_total * jnp.exp(logits - log_total)
        for k in range(top):
            grad = grad + jnp.where(
                spot_ref[:, top + k:top + k + 1] == lanes, probs[k] * (scores[k] - mean), 0.0
            )
        lref[mine, :] = grad.astype(BF16)
        start_own((LOGIT,))

    def token_grads():
        for k in range(1, flight):
            give_dx(k, from_peer(k)).wait_recv()
        picks = sum(one_hot(k).astype(F32) for k in range(top)).astype(BF16)
        own_lg = lref[mine, :]
        for col in range(0, width, wide):
            total = jnp.dot(picks, home_dx[:, col:col + wide], preferred_element_type=F32)
            total = total + lax.dot_general(
                own_lg, rw_ref[col:col + wide, :], (((1,), (1,)), ((), ())),
                preferred_element_type=F32,
            )
            tg_ref[:, col:col + wide] = total.astype(BF16)

    def router(group):
        wait_sibling(group, (LOGIT,))
        load_x(group).wait()
        rows = pl.ds(pl.multiple_of(group * rows_group, rows_group), rows_group)
        grad = lref[rows, :].astype(F32).T.astype(BF16)
        for col in range(0, width, wide):
            rgt[:, col:col + wide] += jnp.dot(
                grad, xb[:, col:col + wide], preferred_element_type=F32
            )

    tiles = hidden_units // tile

    def step(j, carry):
        group = group_at(j)
        own = j == 0
        late_half = j >= copies // 2
        early = group_at(jnp.maximum(2 * (j - copies // 2), 0))
        second = group_at(jnp.maximum(2 * (j - copies // 2) + 1, 0))

        def events(chunk):
            for k in range(copies):
                if slots[k][chunk]:
                    @pl.when(j == k)
                    def _():
                        for event in slots[k][chunk]:
                            handle(event)

        events(0)

        @pl.when(own)
        def _():
            own_x.wait()
            own_o.wait()

        gather_rows(group)

        @pl.when(late_half)
        def _():
            load_x(early).start()

        @pl.when(own)
        def _():
            load_g.wait()
            load_d.wait()

        for index in range(tiles):
            events(1 + index)
            hidden_tile(index * tile, own)
        events(1 + tiles)
        weight_grads()
        events(2 + tiles)
        pl.when(j == 0)(send_scores)
        pl.when(j == 1)(logit_grads)
        pl.when(j == 2)(token_grads)

        @pl.when(late_half)
        def _():
            router(early)
            load_x(second).start()

        events(3 + tiles)
        pl.when(j == 0)(send_rows)

        @pl.when(late_half)
        def _():
            router(second)

        return carry

    lax.fori_loop(0, copies, step, 0)
    for event in late:
        handle(event)
    gu_ref[0] = acc_gu[...].astype(BF16)
    dn_ref[0] = acc_dn[pl.ds(dn_off, dn_rows), :].astype(BF16)
    rout_ref[...] = rgt[...].T
    for part, js in sorted({key[:2] for key in sites.index}):
        each(part, js, lambda copy: copy.wait_send())
    for k in range(1, flight):
        give_score(k, e).wait_send()
        give_dx(k, e).wait_send()


def finish_kernel(*refs):
    for source, target in zip(refs[:4], refs[4:]):
        target[...] = source[...]


def per_device(tokens, out_grad, z_weight, router_weight, expert_ids, gate_up_weight, down_weight):
    n = lax.axis_size("dp")
    flight = lax.axis_size("expert")
    w_gateup, w_down = gate_up_weight[0], down_weight[0]
    tok_count, width = tokens.shape
    routed = router_weight.shape[1]
    hidden = w_down.shape[0]
    gate_up = w_gateup.shape[1]
    cap = tok_count // 2
    rows = flight * cap
    gu_rows, dn_rows = width // n, hidden // n
    window = min(hidden, (dn_rows + 127) // 128 * 128 + 128)
    if dn_rows % 128 == 0:
        window = dn_rows
    elif dn_rows + (128 - math.gcd(dn_rows, 128)) <= window - 128:
        window -= 128
    grid = grid_of(n, flight)
    parts = make_parts(grid, tok_count)
    sites = Sites(grid, parts)
    sizes = [p[2] * width * 2 for p in parts]
    sizes[-2], sizes[-1] = 8 * flight * tok_count, 2 * tok_count * routed
    starts = [0.0] * (len(parts) - 2) + [4.0, 50.0]
    tiles = hidden // min(hidden, 512)
    base = [2.8] + [2.2] * tiles + [1.8]
    chunk_times = [
        base + ([2.5, 2.5] if j == 0 else [2.0, 0.0] if j < 3 else [0.0, 0.0] if j < n // 2 else [1.3, 1.3])
        for j in range(n)
    ]
    send_slot = (1, 2 + tiles)
    slots, late = make_plan(grid, parts, sizes, starts, chunk_times, send_slot)
    dma = pltpu.SemaphoreType.DMA
    vmem = pl.BlockSpec(memory_space=pltpu.VMEM)
    hbm = pl.BlockSpec(memory_space=pl.ANY)
    shape = jax.ShapeDtypeStruct
    blocks = n * flight
    gate_up_grad, down_grad, router_grad, token_grad, _, _ = pl.pallas_call(
        functools.partial(
            layer_kernel, n, flight, cap, grid, parts, sites, slots, late, send_slot
        ),
        out_shape=(
            shape((1, gu_rows, gate_up), BF16),
            shape((1, dn_rows, width), BF16),
            shape((width, routed), F32),
            shape((tok_count, width), BF16),
            shape((blocks * tok_count, width), BF16),
            shape((blocks * tok_count, width), BF16),
        ),
        in_specs=[vmem] * 5 + [hbm] * 2,
        out_specs=(vmem,) * 4 + (hbm,) * 2,
        scratch_shapes=[
            pltpu.VMEM(w_gateup.shape, BF16),
            pltpu.VMEM(w_down.shape, BF16),
            pltpu.VMEM((flight * tok_count, width), BF16),
            pltpu.VMEM((flight * tok_count, width), BF16),
            pltpu.VMEM((rows, width), BF16),
            pltpu.VMEM((rows, width), BF16),
            pltpu.VMEM((rows, 128), F32),
            pltpu.VMEM((rows, gate_up), BF16),
            pltpu.VMEM((rows, hidden), BF16),
            pltpu.VMEM((gu_rows, gate_up), F32),
            pltpu.VMEM((window, width), F32),
            pltpu.VMEM((tok_count, routed), F32),
            pltpu.VMEM((tok_count, routed), F32),
            pltpu.VMEM((tok_count, routed), jnp.int32),
            pltpu.VMEM((blocks, 2 * flight, tok_count), F32),
            pltpu.VMEM((blocks * tok_count, routed), BF16),
            pltpu.VMEM((routed, width), F32),
            pltpu.VMEM((rows, width), BF16),
            pltpu.VMEM((rows, width), BF16),
            pltpu.VMEM((rows, routed), F32),
            pltpu.VMEM((flight, cap, routed), F32),
            dma, dma, dma((2,)), dma((2,)),
            dma((len(sites.index),)), dma((len(parts), blocks)),
        ] + [dma((flight - 1,))] * 4,
        compiler_params=pltpu.CompilerParams(
            collective_id=0, has_side_effects=True, vmem_limit_bytes=67_000_000
        ),
        name="layer",
    )(
        tokens,
        out_grad,
        router_weight,
        expert_ids.T,
        z_weight[None, :],
        w_gateup,
        w_down,
    )
    results = (token_grad, router_grad, gate_up_grad, down_grad)
    return pl.pallas_call(
        finish_kernel,
        out_shape=tuple(shape(r.shape, r.dtype) for r in results),
        in_specs=[vmem] * 4,
        out_specs=(vmem,) * 4,
        compiler_params=pltpu.CompilerParams(vmem_limit_bytes=16 * 2**20),
        name="finish",
    )(*results)


def solution(mesh):
    return jax.shard_map(
        per_device,
        mesh=mesh,
        in_specs=(
            P(("dp", "expert"), None),
            P(("dp", "expert"), None),
            P(("dp", "expert")),
            P(),
            P(("dp", "expert"), None),
            P("expert", None, None),
            P("expert", None, None),
        ),
        out_specs=(
            P(("dp", "expert"), None),
            P(),
            P("expert", "dp", None),
            P("expert", "dp", None),
        ),
        check_vma=False,
    )
```

time: 233 us -> 207 us (0.89)
  Pallas kernels: 227 us -> 200 us
    pallas_call x1, Pallas kernels: 225 us -> 198 us  [per_device(): pl.pallas_call(functools.partial(layer_kernel, n, flight, cap, grid, part...]
where the time goes in v1:
time: 207 us; the launch traced here: 206 us
  Pallas kernels  200 us (97%)
  local copies, waits for them, and re-layouts  4.8 us (2%)
    pallas_call x1, Pallas kernels, per_device(): pl.pallas_call(functools.partial(layer_kernel, n, flight, cap, grid, part...  198 us
    unnamed x8, local copies, waits for them, and re-layouts  4.8 us

profile of v1, /device:TPU:0, one launch (start us, length us, event | category | flops | bytes accessed | tf_op | source)
XLA Modules:
  0.0 205.8 jit_solution(8165233078565610302)
XLA Ops:
  0.6 198.1 %layer.1 = (bf16[1,256,3072]{2,1,0:T(8,128)(2,1)}, bf16[1,192,2048]{2,1,0:T(8,128)(2,1)}, f32[2048,128]{1,0:T(8,128)}, bf16[128,2048]{1,0:T(8,128)(2,1)}, bf16[4...) custom-call(bf16[128,2048]{1,0:T(8,128)(2,1)} %refs_0_.1, bf16[128,2048]{1,0:T(8,128)(2,1)} %refs_1_.1, ...), custom_call_target="tpu_custom_call" | custom-call | tf_op jit(solution)/shard_map/layer/pallas_call | solution.py:632
  198.8 0.0 copy-start
  198.8 1.4 copy-done
  200.2 0.0 copy-start.1
  200.2 1.2 copy-done.1
  201.4 0.0 copy-start.2
  201.4 1.1 copy-done.2
  202.5 0.0 copy-start.3
  202.6 1.0 copy-done.3
  203.6 2.2 %finish.1 = (bf16[128,2048]{1,0:T(8,128)(2,1)}, f32[2048,128]{1,0:T(8,128)}, bf16[1,256,3072]{2,1,0:T(8,128)(2,1)}, bf16[1,192,2048]{2,1,0:T(8,128)(2,1)}) custom-call(bf16[128,2048]{1,0:T(8,128)(2,1)S(1)} %copy-done.3, f32[2048,128]{1,0:T(8,128)S(1)} %copy-done.1, bf16[1,256,3072]{2,1,0:T(8,128)(2,1)S(1)} %copy-done, bf16[1,192,2048]{2,1,0:T(8,128)(2,1)S(1)} %copy-done.2), custom_call_target="tpu_custom_call" | custom-call | tf_op jit(solution)/shard_map/finish/pallas_call | solution.py:685
Async XLA Ops:
  198.8 1.4 copy-start
  200.2 1.2 copy-start.1
  201.4 1.1 copy-start.2
  202.5 1.0 copy-start.3

commit v2 on v1

--- a/solution.py
+++ b/solution.py
@@ -16,6 +16,11 @@
 TOKENS, COTANGENTS, META, LOGIT = range(4)
 LINK_RATE = 46.6e3
 LINK_DELAY = 3.0
+EVENT_TIME = 0.25
+SEND_TIME = 0.05
+LINK_DEPTH = 6.0
+META_TIME = 4.0
+ALL = "all"
 
 
 def lookup(table, key):
@@ -33,7 +38,7 @@
 
 def visit_order(size):
     return [
-        [i] + sorted((k for k in range(size) if k != i), key=lambda k: (abs(k - i), k < i))
+        [i] + sorted((k for k in range(size) if k != i), key=lambda k: (abs(k - i), abs(2 * k + 1 - size)))
         for i in range(size)
     ]
 
@@ -71,7 +76,7 @@
     return found
 
 
-def mean_arrivals(grid, parts, sizes, starts):
+def mean_arrivals(grid, parts, sizes):
     dims = list(grid)
     visits = {d: visit_order(grid[d]) for d in dims}
     nodes = [dict(zip(dims, at)) for at in itertools.product(*[range(grid[d]) for d in dims])]
@@ -88,7 +93,7 @@
 
     for part in range(len(parts)):
         for here in nodes:
-            heapq.heappush(queue, (starts[part], next(count), here, part, here))
+            heapq.heappush(queue, (0.0, next(count), here, part, here))
     while queue:
         time, _, here, part, source = heapq.heappop(queue)
         if source != here:
@@ -98,38 +103,163 @@
     return {key: sum(found) / len(found) for key, found in times.items()}
 
 
-def make_plan(grid, parts, sizes, starts, chunk_times, send_slot):
-    arrivals = sorted((time, key) for key, time in mean_arrivals(grid, parts, sizes, starts).items())
-    groups, chunks = len(chunk_times), len(chunk_times[0])
-    last = {}
-    for index, (_, (part, (jz, jx, jy))) in enumerate(arrivals):
-        if parts[part][0] != LOGIT:
-            last[jz * grid["x"] + jx] = index
-    router_from = groups // 2
-    for index, (_, (part, (jz, jx, jy))) in enumerate(arrivals):
-        if parts[part][0] == LOGIT:
-            user = router_from + (jz * grid["x"] + jx) // 2
-            last[user] = max(last.get(user, -1), index)
-    slots = [[[] for _ in range(chunks)] for _ in range(groups)]
-    late, now, done, held = [], 0.0, 0, []
-    for group in range(groups):
-        for chunk in range(chunks):
-            here = slots[group][chunk]
-            sent = (group, chunk) > send_slot
-            if sent and held:
-                here += held
-                held = []
-            while done < len(arrivals) and (arrivals[done][0] <= now or done <= last.get(group, -1)):
-                time, key = arrivals[done]
-                if parts[key[0]][0] == LOGIT and not sent:
-                    held.append(key)
-                else:
-                    here.append(key)
-                now = max(now, time)
-                done += 1
-            now += chunk_times[group][chunk]
-    late = held + [key for _, key in arrivals[done:]]
-    return slots, late
+def make_plan(grid, parts, sizes, times, share_slot, router_from):
+    dims = list(grid)
+    visits = {d: visit_order(grid[d]) for d in dims}
+    nodes = [dict(zip(dims, at)) for at in itertools.product(*[range(grid[d]) for d in dims])]
+    number = {tuple(node.values()): i for i, node in enumerate(nodes)}
+    groups, chunks = len(times), len(times[0])
+    wanted = {}
+    for part, (kind, *_) in enumerate(parts):
+        for js in itertools.product(*[range(grid[d]) for d in dims]):
+            if any(js):
+                key = (kind == LOGIT, js[0] * grid["x"] + js[1])
+                wanted.setdefault(key, set()).add((part, js))
+    queue, free, count = [], {}, itertools.count()
+    ready = [[] for _ in nodes]
+    waiting = [{} for _ in nodes]
+    seen = [set() for _ in nodes]
+    at_slot = [0] * len(nodes)
+    asleep = [False] * len(nodes)
+    trace = [[] for _ in nodes]
+    taken = [[] for _ in nodes]
+
+    def push(time, what, node, *rest):
+        heapq.heappush(queue, (round(time, 3), what > 0, next(count), what, node) + rest)
+
+    def offer(node, part, source):
+        here = nodes[node]
+        js = tuple(visits[d][here[d]].index(source[d]) for d in dims)
+        for d, way in routes(grid, parts[part][3], source, here):
+            small = parts[part][0] in (META, LOGIT)
+            entry = (not small, js[0], part, js, source)
+            heapq.heappush(waiting[node].setdefault((d, way), []), entry)
+
+    def own(node, kinds):
+        for part, (kind, *_) in enumerate(parts):
+            if kind in kinds:
+                offer(node, part, nodes[node])
+
+    def startable(node, slot):
+        if slot == 0:
+            return True
+        if slot > groups * chunks:
+            return False
+        group, chunk = divmod(slot - 1, chunks)
+        if chunk == 0:
+            for g in range(groups):
+                if g not in taken[node] and wanted.get((False, g), set()) <= seen[node]:
+                    taken[node].append(g)
+                    return True
+            return False
+        if group >= router_from and chunk >= chunks - 2:
+            user = taken[node][2 * (group - router_from) + chunk - chunks + 2]
+            return wanted.get((True, user), set()) <= seen[node]
+        return True
+
+    for node in range(len(nodes)):
+        own(node, (TOKENS, COTANGENTS))
+        push(0.0, 1, node)
+    while queue:
+        time, _, _, what, node, *rest = heapq.heappop(queue)
+        here = nodes[node]
+        if what == 0:
+            part, source = rest
+            js = tuple(visits[d][here[d]].index(source[d]) for d in dims)
+            heapq.heappush(ready[node], (js[0], time, part, js, source))
+        if what in (0, 4):
+            if asleep[node]:
+                asleep[node] = False
+                push(time, 1, node)
+            continue
+        if what == 2:
+            own(node, (META,))
+        if what == 3:
+            own(node, (LOGIT,))
+        slot = at_slot[node]
+        if ready[node]:
+            _, _, part, js, source = heapq.heappop(ready[node])
+            seen[node].add((part, js))
+            trace[node].append((slot, (part, js, None)))
+            offer(node, part, source)
+            push(time + EVENT_TIME, 1, node)
+            continue
+        open_links = [
+            (entries[0], link) for link, entries in waiting[node].items()
+            if entries and free.get((node, link), 0.0) - time < LINK_DEPTH
+        ]
+        if open_links:
+            turned = {d: -1 if 2 * here[d] >= grid[d] else 1 for d in dims}
+            _, link = min(
+                open_links, key=lambda one: (one[0][:4], one[1][0], -one[1][1] * turned[one[1][0]])
+            )
+            _, _, part, js, source = heapq.heappop(waiting[node][link])
+            trace[node].append((slot, (part, js, link)))
+            end = max(time, free.get((node, link), 0.0)) + sizes[part] / LINK_RATE
+            free[(node, link)] = end
+            there = dict(here)
+            there[link[0]] += link[1]
+            push(end + LINK_DELAY, 0, number[tuple(there.values())], part, source)
+            push(time + SEND_TIME, 1, node)
+            continue
+        if startable(node, slot):
+            at_slot[node] += 1
+            if slot == 0:
+                push(time + META_TIME, 2, node)
+            else:
+                group, chunk = divmod(slot - 1, chunks)
+                push(time + times[group][chunk], 3 if slot == share_slot else 1, node)
+            continue
+        asleep[node] = True
+        wake = [free[(node, link)] - LINK_DEPTH for link, entries in waiting[node].items() if entries]
+        if wake:
+            push(max(min(wake), time) + 0.01, 4, node)
+    return nodes, trace, taken, time
+
+
+def mirrored(grid, node, plan):
+    flips = {d for d in grid if 2 * node[d] >= grid[d]}
+    return [
+        (at, (part, js, link and (link[0], -link[1] if link[0] in flips else link[1])))
+        for at, (part, js, link) in plan
+    ]
+
+
+def make_slots(grid, parts, sizes, times, share_slot, router_from):
+    nodes, trace, taken, _ = make_plan(grid, parts, sizes, times, share_slot, router_from)
+    groups = len(times)
+    flat = [mirrored(grid, node, plan) for node, plan in zip(nodes, trace)]
+    kinds = [min(node["z"], grid["z"] - 1 - node["z"]) for node in nodes]
+    known = sorted(set(kinds))
+    firsts = [kinds.index(kind) for kind in known]
+    same = all(
+        sorted(map(repr, flat[i])) == sorted(map(repr, flat[firsts[known.index(kind)]]))
+        and taken[i] == taken[firsts[known.index(kind)]]
+        for i, kind in enumerate(kinds)
+    )
+    if same and max(grid["x"], grid["y"]) <= 2:
+        table = [known.index(min(z, grid["z"] - 1 - z)) for z in range(grid["z"])]
+        plans = [flat[i] for i in firsts]
+        orders = [taken[i] for i in firsts]
+    else:
+        table, orders = [0] * grid["z"], [list(range(groups))]
+        arrivals = mean_arrivals(grid, parts, sizes)
+        plan = []
+        for kinds_now, at in (((TOKENS, COTANGENTS), 0), ((META,), 1), ((LOGIT,), share_slot + 1)):
+            for part, (kind, *_) in enumerate(parts):
+                if kind in kinds_now:
+                    plan.append((at, (part, (0, 0, 0), ALL)))
+        for _, (part, js) in sorted((time, key) for key, time in arrivals.items()):
+            at = share_slot + 1 if parts[part][0] == LOGIT else 1
+            plan += [(at, (part, js, None)), (at, (part, js, ALL))]
+        plans = [plan]
+    slots = []
+    for plan in plans:
+        found = {}
+        for at, action in plan:
+            found.setdefault(at, []).append(action)
+        slots.append(found)
+    return table, slots, orders
 
 
 class Sites:
@@ -157,10 +287,10 @@
         return [key[2] for key in self.index if key[0] == part and key[1] == js]
 
 
-def layer_kernel(copies, flight, cap, grid, parts, sites, slots, late, send_slot, *refs):
+def layer_kernel(copies, flight, cap, grid, parts, sites, table, slots, orders, chunks, *refs):
     (tok_ref, og_ref, rw_ref, ids_ref, zw_ref, wg_hbm, wd_hbm,
      gu_ref, dn_ref, rout_ref, tg_ref, gx, go,
-     wg_ref, wd_ref, xb, ob, rows_x, rows_o, prob_ref, pg_ref, hid, acc_gu, acc_dn,
+     wg_ref, wd_ref, xb, ob, rows_x, rows_o, prob_ref, gate_ref, up_ref, pg_ref, hid, acc_gu, acc_dn,
      logit_ref, small_ref, spot_ref, mref, lref, rgt, back, home_dx, score_ref, home_score,
      wg_sem, wd_sem, own_sem, load_sem, send_sem, recv_sem,
      sc_send, sc_recv, dx_send, dx_recv) = refs
@@ -190,6 +320,8 @@
         return dp * flight + expert
 
     me = block_index(my, core)
+    my_kind = lookup(table, my["z"])
+    my_flip = 2 * my["z"] >= grid["z"]
 
     def slice_of(part, index, own=False):
         kind, start, rows, _ = parts[part]
@@ -244,18 +376,48 @@
             else:
                 pl.when(guard)(functools.partial(act, copy))
 
-    def handle(event):
-        part, js = event
-        at = {k: coord[k][j] for k, j in zip(dims, js)}
-        arrival(part, block_index(at, core)).wait_recv()
-        each(part, js, lambda copy: copy.start())
+    def launch(part, js, wanted):
+        for kind in sites.of(part, js):
+            if not wanted(kind):
+                continue
+            guard, copy = outgoing(part, js, kind)
+            if guard is None:
+                copy.start()
+            else:
+                pl.when(guard)(copy.start)
+
+    def handle(action, flipped):
+        part, js, link = action
+        if link is None:
+            at = {k: coord[k][j] for k, j in zip(dims, js)}
+            arrival(part, block_index(at, core)).wait_recv()
+            launch(part, js, lambda kind: kind[0] == "core")
+        elif link == ALL:
+            launch(part, js, lambda kind: kind[0] != "core")
+        elif grid[link[0]] > 2 and not js[dims.index(link[0])]:
+            pl.when(flipped)(lambda: launch(part, js, lambda kind: kind == (link[0], -link[1])))
+            pl.when(~flipped)(lambda: launch(part, js, lambda kind: kind == link))
+        else:
+            launch(part, js, lambda kind: kind[0] == link[0])
+
+    def run_actions(slot, when=None):
+        for kind, found in enumerate(slots):
+            if slot in found:
+                here = my_kind == kind
+                if when is not None:
+                    here = here & when
+
+                @pl.when(here)
+                def _():
+                    for action in found[slot]:
+                        handle(action, my_flip)
 
     home = (0,) * len(dims)
 
     def start_own(kinds):
         for part, (kind, *_) in enumerate(parts):
             if kind in kinds:
-                each(part, home, lambda copy: copy.start())
+                launch(part, home, lambda kind: kind[0] == "core")
 
     barrier = pltpu.get_barrier_semaphore()
     for k in range(1, flight):
@@ -287,6 +449,7 @@
     own_x.start()
     own_o.start()
     pl.semaphore_wait(barrier, greeted)
+    run_actions(0)
     start_own((TOKENS, COTANGENTS))
 
     lanes = lax.broadcasted_iota(jnp.int32, (tok_count, routed), 1)
@@ -337,7 +500,8 @@
     dn_start = pl.multiple_of(dn_start, 128)
 
     def group_at(j):
-        jz, jx = lax.div(j, grid["x"]), lax.rem(j, grid["x"])
+        g = lookup(sum(orders, []), my_kind * copies + j)
+        jz, jx = lax.div(g, grid["x"]), lax.rem(g, grid["x"])
         z = lookup(sum(visits["z"], []), my["z"] * grid["z"] + jz)
         x = lookup(sum(visits["x"], []), my["x"] * grid["x"] + jx)
         return z * grid["x"] + x
@@ -357,38 +521,57 @@
         rows = pl.ds(pl.multiple_of(group * rows_group, rows_group), rows_group)
         return pltpu.make_async_copy(go.at[rows, :], ob, load_sem.at[1])
 
-    ranks = lax.broadcasted_iota(jnp.int32, (cap, tok_count), 0).astype(F32)
-
-    def gather_rows(group):
+    ranks = lax.broadcasted_iota(jnp.int32, (2 * cap, 2 * tok_count), 0).astype(F32)
+
+    def pair_rank(group, pair):
+        index = group * flight + 2 * pair
+        first = mref[index, pl.ds(e, 1), :]
+        second = mref[index + 1, pl.ds(e, 1), :]
+        second = jnp.where(second >= 0.0, second + float(cap), -1.0)
+        return jnp.concatenate([first, second], axis=1) == ranks
+
+    def pick_rows(group, source, target):
+        for pair in range(flight // 2):
+            picks = pair_rank(group, pair).astype(F32).astype(BF16)
+            target[pair * 2 * cap:(pair + 1) * 2 * cap, :] = jnp.dot(
+                picks, source[pair * 2 * tok_count:(pair + 1) * 2 * tok_count, :],
+                preferred_element_type=F32,
+            ).astype(BF16)
+
+    def gather_x(group):
         wait_sibling(group, (TOKENS, COTANGENTS, META))
         load_x(group).start()
         load_o(group).start()
-        picks = []
-        for s in range(flight):
-            index = group * flight + s
-            pick = mref[index, pl.ds(e, 1), :] == ranks
-            part = jnp.where(pick, mref[index, pl.ds(flight + e, 1), :], 0.0)
+        for pair in range(flight // 2):
+            index = group * flight + 2 * pair
+            weights = jnp.concatenate(
+                [mref[index + i, pl.ds(flight + e, 1), :] for i in range(2)], axis=1
+            )
+            part = jnp.where(pair_rank(group, pair), weights, 0.0)
             prob = jnp.sum(part, axis=1, keepdims=True)
-            prob_ref[s * cap:(s + 1) * cap, :] = jnp.broadcast_to(prob, (cap, prob_ref.shape[1]))
-            picks.append(pick.astype(F32).astype(BF16))
+            prob_ref[pair * 2 * cap:(pair + 1) * 2 * cap, :] = jnp.broadcast_to(
+                prob, (2 * cap, prob_ref.shape[1])
+            )
         load_x(group).wait()
+        pick_rows(group, xb, rows_x)
+
+    def gather_o(group):
         load_o(group).wait()
-        for s in range(flight):
-            rows = slice(s * cap, (s + 1) * cap)
-            toks = slice(s * tok_count, (s + 1) * tok_count)
-            rows_x[rows, :] = jnp.dot(
-                picks[s], xb[toks, :], preferred_element_type=F32
-            ).astype(BF16)
-            rows_o[rows, :] = jnp.dot(
-                picks[s], ob[toks, :], preferred_element_type=F32
-            ).astype(BF16)
-
-    def hidden_tile(col, own):
-        gate = jnp.dot(rows_x[...], wg_ref[:, col:col + tile], preferred_element_type=F32)
-        up = jnp.dot(
+        pick_rows(group, ob, rows_o)
+
+    def gate_tile(col):
+        gate_ref[...] = jnp.dot(
+            rows_x[...], wg_ref[:, col:col + tile], preferred_element_type=F32
+        )
+
+    def up_tile(col):
+        up_ref[...] = jnp.dot(
             rows_x[...], wg_ref[:, hidden_units + col:hidden_units + col + tile],
             preferred_element_type=F32,
         )
+
+    def hidden_tile(col, own):
+        gate, up = gate_ref[...], up_ref[...]
         raw = lax.dot_general(
             rows_o[...], wd_ref[col:col + tile, :], (((1,), (1,)), ((), ())),
             preferred_element_type=F32,
@@ -407,7 +590,7 @@
             part = jnp.broadcast_to(part, score_ref.shape)
             score_ref[...] = part if col == 0 else score_ref[...] + part
 
-    def weight_grads():
+    def up_grads():
         rows_o[...] = (prob_ref[:, 0:1] * rows_o[...].astype(F32)).astype(BF16)
         taken = rows_x[:, pl.ds(pl.multiple_of(d * gu_rows, gu_rows), gu_rows)]
         for col in range(0, 2 * hidden_units, tile):
@@ -415,6 +598,8 @@
                 taken, pg_ref[:, col:col + tile], (((0,), (0,)), ((), ())),
                 preferred_element_type=F32,
             )
+
+    def down_grads():
         taken = hid[:, pl.ds(dn_start, window)]
         for col in range(0, width, wide):
             acc_dn[:, col:col + wide] += lax.dot_general(
@@ -526,59 +711,64 @@
         early = group_at(jnp.maximum(2 * (j - copies // 2), 0))
         second = group_at(jnp.maximum(2 * (j - copies // 2) + 1, 0))
 
-        def events(chunk):
+        spot_now = [0]
+
+        def then(run):
+            chunk = spot_now[0]
+            spot_now[0] += 1
             for k in range(copies):
-                if slots[k][chunk]:
-                    @pl.when(j == k)
-                    def _():
-                        for event in slots[k][chunk]:
-                            handle(event)
-
-        events(0)
-
-        @pl.when(own)
-        def _():
-            own_x.wait()
-            own_o.wait()
-
-        gather_rows(group)
-
-        @pl.when(late_half)
-        def _():
-            load_x(early).start()
-
-        @pl.when(own)
-        def _():
-            load_g.wait()
-            load_d.wait()
-
+                run_actions(1 + k * chunks + chunk, j == k)
+            run()
+
+        def first_rows():
+            @pl.when(own)
+            def _():
+                own_x.wait()
+                own_o.wait()
+
+            gather_x(group)
+
+            @pl.when(late_half)
+            def _():
+                load_x(early).start()
+
+            @pl.when(own)
+            def _():
+                load_g.wait()
+                load_d.wait()
+
+        then(first_rows)
+        then(lambda: gather_o(group))
         for index in range(tiles):
-            events(1 + index)
-            hidden_tile(index * tile, own)
-        events(1 + tiles)
-        weight_grads()
-        events(2 + tiles)
-        pl.when(j == 0)(send_scores)
-        pl.when(j == 1)(logit_grads)
-        pl.when(j == 2)(token_grads)
-
-        @pl.when(late_half)
-        def _():
-            router(early)
-            load_x(second).start()
-
-        events(3 + tiles)
-        pl.when(j == 0)(send_rows)
-
-        @pl.when(late_half)
-        def _():
-            router(second)
-
+            then(functools.partial(gate_tile, index * tile))
+            then(functools.partial(up_tile, index * tile))
+            then(functools.partial(hidden_tile, index * tile, own))
+        then(up_grads)
+        then(down_grads)
+
+        def special():
+            pl.when(j == 0)(send_scores)
+            pl.when(j == 1)(logit_grads)
+            pl.when(j == 2)(token_grads)
+
+            @pl.when(late_half)
+            def _():
+                router(early)
+                load_x(second).start()
+
+        def special_late():
+            pl.when(j == 0)(send_rows)
+
+            @pl.when(late_half)
+            def _():
+                router(second)
+
+        then(special)
+        then(special_late)
         return carry
 
     lax.fori_loop(0, copies, step, 0)
-    for event in late:
-        handle(event)
+    run_actions(1 + copies * chunks)
     gu_ref[0] = acc_gu[...].astype(BF16)
     dn_ref[0] = acc_dn[pl.ds(dn_off, dn_rows), :].astype(BF16)
     rout_ref[...] = rgt[...].T
@@ -590,8 +780,22 @@
 
 
 def finish_kernel(*refs):
-    for source, target in zip(refs[:4], refs[4:]):
-        target[...] = source[...]
+    sources, targets, holds, sems = refs[:4], refs[4:8], refs[8:12], refs[12]
+    takes = [
+        pltpu.make_async_copy(source, hold, sems.at[i])
+        for i, (source, hold) in enumerate(zip(sources, holds))
+    ]
+    gives = [
+        pltpu.make_async_copy(hold, target, sems.at[4 + i])
+        for i, (hold, target) in enumerate(zip(holds, targets))
+    ]
+    for take in takes:
+        take.start()
+    for take, give in zip(takes, gives):
+        take.wait()
+        give.start()
+    for give in gives:
+        give.wait()
 
 
 def per_device(tokens, out_grad, z_weight, router_weight, expert_ids, gate_up_weight, down_weight):
@@ -615,15 +819,15 @@
     sites = Sites(grid, parts)
     sizes = [p[2] * width * 2 for p in parts]
     sizes[-2], sizes[-1] = 8 * flight * tok_count, 2 * tok_count * routed
-    starts = [0.0] * (len(parts) - 2) + [4.0, 50.0]
     tiles = hidden // min(hidden, 512)
-    base = [2.8] + [2.2] * tiles + [1.8]
+    base = [1.9, 1.0] + [0.57, 0.57, 0.75] * tiles + [0.75, 0.55]
     chunk_times = [
-        base + ([2.5, 2.5] if j == 0 else [2.0, 0.0] if j < 3 else [0.0, 0.0] if j < n // 2 else [1.3, 1.3])
+        base + ([2.0, 2.0] if j == 0 else [1.6, 0.1] if j < 3 else [0.1, 0.1] if j < n // 2 else [1.3, 1.3])
         for j in range(n)
     ]
-    send_slot = (1, 2 + tiles)
-    slots, late = make_plan(grid, parts, sizes, starts, chunk_times, send_slot)
+    chunks = len(base) + 2
+    share_slot = 1 + chunks + len(base)
+    table, slots, orders = make_slots(grid, parts, sizes, chunk_times, share_slot, n // 2)
     dma = pltpu.SemaphoreType.DMA
     vmem = pl.BlockSpec(memory_space=pltpu.VMEM)
     hbm = pl.BlockSpec(memory_space=pl.ANY)
@@ -631,7 +835,7 @@
     blocks = n * flight
     gate_up_grad, down_grad, router_grad, token_grad, _, _ = pl.pallas_call(
         functools.partial(
-            layer_kernel, n, flight, cap, grid, parts, sites, slots, late, send_slot
+            layer_kernel, n, flight, cap, grid, parts, sites, table, slots, orders, chunks
         ),
         out_shape=(
             shape((1, gu_rows, gate_up), BF16),
@@ -651,6 +855,8 @@
             pltpu.VMEM((rows, width), BF16),
             pltpu.VMEM((rows, width), BF16),
             pltpu.VMEM((rows, 128), F32),
+            pltpu.VMEM((rows, min(hidden, 512)), F32),
+            pltpu.VMEM((rows, min(hidden, 512)), F32),
             pltpu.VMEM((rows, gate_up), BF16),
             pltpu.VMEM((rows, hidden), BF16),
             pltpu.VMEM((gu_rows, gate_up), F32),
@@ -685,9 +891,10 @@
     return pl.pallas_call(
         finish_kernel,
         out_shape=tuple(shape(r.shape, r.dtype) for r in results),
-        in_specs=[vmem] * 4,
-        out_specs=(vmem,) * 4,
-        compiler_params=pltpu.CompilerParams(vmem_limit_bytes=16 * 2**20),
+        in_specs=[hbm] * 4,
+        out_specs=(hbm,) * 4,
+        scratch_shapes=[pltpu.VMEM(r.shape, r.dtype) for r in results] + [dma((8,))],
+        compiler_params=pltpu.CompilerParams(vmem_limit_bytes=67_000_000),
         name="finish",
     )(*results)
 

time: 207 us -> 191 us (0.923)
  Pallas kernels: 200 us -> 190 us
  local copies, waits for them, and re-layouts: 4.8 us -> 0 us
    pallas_call x1, Pallas kernels: 198 us -> 186 us  [per_device(): pl.pallas_call(functools.partial(layer_kernel, n, flight, cap, grid, part...]
    unnamed x8 -> x0, local copies, waits for them, and re-layouts: 4.8 us -> none
where the time goes in v2:
time: 191 us; the launch traced here: 190 us
  Pallas kernels  190 us (99%)
    pallas_call x1, Pallas kernels, per_device(): pl.pallas_call(functools.partial(layer_kernel, n, flight, cap, grid, part...  186 us

profile of v2, /device:TPU:0, one launch (start us, length us, event | category | flops | bytes accessed | tf_op | source)
XLA Modules:
  0.0 190.5 jit_solution(13735767704506458818)
XLA Ops:
  0.6 186.5 %layer.1 = (bf16[1,256,3072]{2,1,0:T(8,128)(2,1)}, bf16[1,192,2048]{2,1,0:T(8,128)(2,1)}, f32[2048,128]{1,0:T(8,128)}, bf16[128,2048]{1,0:T(8,128)(2,1)}, bf16[4...) custom-call(bf16[128,2048]{1,0:T(8,128)(2,1)} %refs_0_.1, bf16[128,2048]{1,0:T(8,128)(2,1)} %refs_1_.1, ...), custom_call_target="tpu_custom_call" | custom-call | tf_op jit(solution)/shard_map/layer/pallas_call | solution.py:836
  187.1 3.4 %finish.1 = (bf16[128,2048]{1,0:T(8,128)(2,1)}, f32[2048,128]{1,0:T(8,128)}, bf16[1,256,3072]{2,1,0:T(8,128)(2,1)}, bf16[1,192,2048]{2,1,0:T(8,128)(2,1)}) custom-call(bf16[128,2048]{1,0:T(8,128)(2,1)} %get-tuple-element.8.refs_0_, f32[2048,128]{1,0:T(8,128)} %get-tuple-element.9.refs_1_, bf16[1,256,3072]{2,1,0:T(8,128)(2,1)} %get-tuple-element.10.refs_2_, ...), custom_call_target="tpu_custom_call" | custom-call | tf_op jit(solution)/shard_map/finish/pallas_call | solution.py:891

commit v3 on v2

--- a/solution.py
+++ b/solution.py
@@ -13,14 +13,14 @@
 F32 = jnp.float32
 BF16 = jnp.bfloat16
 MESH = pl.DeviceIdType.MESH
-TOKENS, COTANGENTS, META, LOGIT = range(4)
+TOKENS, BLOCK, META, LOGIT = range(4)
 LINK_RATE = 46.6e3
 LINK_DELAY = 3.0
 EVENT_TIME = 0.25
 SEND_TIME = 0.05
-LINK_DEPTH = 6.0
+LINK_DEPTH = 12.0
 META_TIME = 4.0
-ALL = "all"
+ALL, CORE = "all", "core"
 
 
 def lookup(table, key):
@@ -46,19 +46,16 @@
 def make_parts(grid, tok_count):
     straight, crossed = ("x", "z", "y"), ("y", "z", "x")
     first_x, first_y = ("z", "x", "y"), ("z", "y", "x")
-    if math.prod(grid.values()) > 16 or tok_count % 128:
-        pieces = [(0, tok_count, straight, crossed)]
+    if math.prod(grid.values()) > 16 or tok_count % 64:
+        half = tok_count // 2
+        parts = [(TOKENS, 0, half, straight), (TOKENS, half, half, crossed)]
     else:
-        unit = tok_count // 8
-        pieces = [
-            (0, 3 * unit, first_x, first_y),
-            (3 * unit, 3 * unit, straight, crossed),
-            (6 * unit, 2 * unit, straight, crossed),
+        unit = tok_count // 4
+        parts = [
+            (TOKENS, i * unit, unit, order)
+            for i, order in enumerate((first_x, first_y, straight, crossed))
         ]
-    parts = []
-    for start, rows, order_x, order_o in pieces:
-        parts += [(TOKENS, start, rows, order_x), (COTANGENTS, start, rows, order_o)]
-    return parts + [(META, 0, 0, first_x), (LOGIT, 0, 0, first_x)]
+    return parts + [(BLOCK, 0, 0, first_x), (META, 0, 0, first_x), (LOGIT, 0, 0, first_x)]
 
 
 def routes(grid, order, source, here):
@@ -93,6 +90,8 @@
 
     for part in range(len(parts)):
         for here in nodes:
+            if parts[part][0] == BLOCK:
+                continue
             heapq.heappush(queue, (0.0, next(count), here, part, here))
     while queue:
         time, _, here, part, source = heapq.heappop(queue)
@@ -110,9 +109,10 @@
     number = {tuple(node.values()): i for i, node in enumerate(nodes)}
     groups, chunks = len(times), len(times[0])
     wanted = {}
+    whole = sum(kind == TOKENS for kind, *_ in parts)
     for part, (kind, *_) in enumerate(parts):
         for js in itertools.product(*[range(grid[d]) for d in dims]):
-            if any(js):
+            if any(js) and kind != BLOCK:
                 key = (kind == LOGIT, js[0] * grid["x"] + js[1])
                 wanted.setdefault(key, set()).add((part, js))
     queue, free, count = [], {}, itertools.count()
@@ -158,7 +158,7 @@
         return True
 
     for node in range(len(nodes)):
-        own(node, (TOKENS, COTANGENTS))
+        own(node, (TOKENS,))
         push(0.0, 1, node)
     while queue:
         time, _, _, what, node, *rest = heapq.heappop(queue)
@@ -182,6 +182,8 @@
             seen[node].add((part, js))
             trace[node].append((slot, (part, js, None)))
             offer(node, part, source)
+            if parts[part][0] == TOKENS and all((i, js) in seen[node] for i in range(whole)):
+                trace[node].append((slot, (whole, js, CORE)))
             push(time + EVENT_TIME, 1, node)
             continue
         open_links = [
@@ -220,7 +222,7 @@
 def mirrored(grid, node, plan):
     flips = {d for d in grid if 2 * node[d] >= grid[d]}
     return [
-        (at, (part, js, link and (link[0], -link[1] if link[0] in flips else link[1])))
+        (at, (part, js, link if link in (None, CORE) else (link[0], -link[1] if link[0] in flips else link[1])))
         for at, (part, js, link) in plan
     ]
 
@@ -244,14 +246,18 @@
     else:
         table, orders = [0] * grid["z"], [list(range(groups))]
         arrivals = mean_arrivals(grid, parts, sizes)
-        plan = []
-        for kinds_now, at in (((TOKENS, COTANGENTS), 0), ((META,), 1), ((LOGIT,), share_slot + 1)):
+        plan, come = [], {}
+        for kinds_now, at in (((TOKENS,), 0), ((META,), 1), ((LOGIT,), share_slot + 1)):
             for part, (kind, *_) in enumerate(parts):
                 if kind in kinds_now:
                     plan.append((at, (part, (0, 0, 0), ALL)))
         for _, (part, js) in sorted((time, key) for key, time in arrivals.items()):
             at = share_slot + 1 if parts[part][0] == LOGIT else 1
             plan += [(at, (part, js, None)), (at, (part, js, ALL))]
+            if parts[part][0] == TOKENS:
+                come[js] = come.get(js, 0) + 1
+                if come[js] == len(parts) - 3:
+                    plan.append((at, (len(parts) - 3, js, CORE)))
         plans = [plan]
     slots = []
     for plan in plans:
@@ -264,10 +270,11 @@
 
 class Sites:
     def __init__(self, grid, parts):
-        self.index = {}
+        self.index, self.shared = {}, {}
+        own = len(parts)
         visits = [range(grid[d]) for d in grid]
         dims = list(grid)
-        for part, (_, _, _, order) in enumerate(parts):
+        for part, (kind_of, _, _, order) in enumerate(parts):
             for js in itertools.product(*visits):
                 at = dict(zip(dims, js))
                 last = max((i for i, d in enumerate(order) if at[d]), default=-1)
@@ -279,9 +286,18 @@
                         kinds.append((d, 0))
                     elif grid[d] > 2:
                         kinds += [(d, 1), (d, -1)]
-                kinds.append(("core", 0))
+                if kind_of == BLOCK:
+                    kinds = []
+                if kind_of != TOKENS:
+                    kinds.append((CORE, 0))
                 for kind in kinds:
-                    self.index[(part, js, kind)] = len(self.index)
+                    if kind[0] == CORE or grid[kind[0]] == 2:
+                        self.index[(part, js, kind)] = part
+                        self.shared[part] = self.shared.get(part, 0) + 1
+                    else:
+                        self.index[(part, js, kind)] = own
+                        own += 1
+        self.total = own
 
     def of(self, part, js):
         return [key[2] for key in self.index if key[0] == part and key[1] == js]
@@ -289,7 +305,7 @@
 
 def layer_kernel(copies, flight, cap, grid, parts, sites, table, slots, orders, chunks, *refs):
     (tok_ref, og_ref, rw_ref, ids_ref, zw_ref, wg_hbm, wd_hbm,
-     gu_ref, dn_ref, rout_ref, tg_ref, gx, go,
+     gu_ref, dn_ref, rout_ref, tg_ref, gathered,
      wg_ref, wd_ref, xb, ob, rows_x, rows_o, prob_ref, gate_ref, up_ref, pg_ref, hid, acc_gu, acc_dn,
      logit_ref, small_ref, spot_ref, mref, lref, rgt, back, home_dx, score_ref, home_score,
      wg_sem, wd_sem, own_sem, load_sem, send_sem, recv_sem,
@@ -323,18 +339,15 @@
     my_kind = lookup(table, my["z"])
     my_flip = 2 * my["z"] >= grid["z"]
 
-    def slice_of(part, index, own=False):
+    def slice_of(part, index):
         kind, start, rows, _ = parts[part]
         if kind == META:
             return mref.at[index]
         if kind == LOGIT:
             return lref.at[pl.ds(pl.multiple_of(index * tok_count, tok_count), tok_count), :]
-        if own:
-            return (tok_ref if kind == TOKENS else og_ref).at[pl.ds(start, rows), :]
-        unit = math.gcd(start, tok_count) if start else tok_count
-        return (gx if kind == TOKENS else go).at[
-            pl.ds(pl.multiple_of(index * tok_count + start, unit), rows), :
-        ]
+        if kind == BLOCK:
+            return gathered.at[index]
+        return gathered.at[index, :, pl.ds(start, rows), :]
 
     def arrival(part, index):
         there = slice_of(part, index)
@@ -347,7 +360,7 @@
         at = {k: coord[k][j] for k, j in zip(dims, js)}
         dim, way = kind
         target, guard, which = dict(my), None, core
-        if dim == "core":
+        if dim == CORE:
             which = 1 - core
         elif way == 0 and not at[dim] is my[dim] and js[dims.index(dim)]:
             ahead = my[dim] + jnp.where(at[dim] < my[dim], 1, -1)
@@ -362,19 +375,11 @@
         index = block_index(at, core)
         site = sites.index[(part, js, kind)]
         copy = pltpu.make_async_remote_copy(
-            src_ref=slice_of(part, index, own=not any(js)), dst_ref=slice_of(part, index),
+            src_ref=slice_of(part, index), dst_ref=slice_of(part, index),
             send_sem=send_sem.at[site], recv_sem=recv_sem.at[part, index],
             device_id=place(target, which), device_id_type=MESH,
         )
         return guard, copy
-
-    def each(part, js, act):
-        for kind in sites.of(part, js):
-            guard, copy = outgoing(part, js, kind)
-            if guard is None:
-                act(copy)
-            else:
-                pl.when(guard)(functools.partial(act, copy))
 
     def launch(part, js, wanted):
         for kind in sites.of(part, js):
@@ -391,33 +396,48 @@
         if link is None:
             at = {k: coord[k][j] for k, j in zip(dims, js)}
             arrival(part, block_index(at, core)).wait_recv()
-            launch(part, js, lambda kind: kind[0] == "core")
+            launch(part, js, lambda kind: kind[0] == CORE)
+        elif link == CORE:
+            launch(part, js, lambda kind: True)
         elif link == ALL:
-            launch(part, js, lambda kind: kind[0] != "core")
+            launch(part, js, lambda kind: kind[0] != CORE)
         elif grid[link[0]] > 2 and not js[dims.index(link[0])]:
             pl.when(flipped)(lambda: launch(part, js, lambda kind: kind == (link[0], -link[1])))
             pl.when(~flipped)(lambda: launch(part, js, lambda kind: kind == link))
         else:
             launch(part, js, lambda kind: kind[0] == link[0])
 
-    def run_actions(slot, when=None):
+    def run_actions(slot):
         for kind, found in enumerate(slots):
             if slot in found:
-                here = my_kind == kind
-                if when is not None:
-                    here = here & when
-
-                @pl.when(here)
+                @pl.when(my_kind == kind)
                 def _():
                     for action in found[slot]:
                         handle(action, my_flip)
 
+    def run_steps(j, chunk):
+        def tree(found, ks):
+            ks = [k for k in ks if 1 + k * chunks + chunk in found]
+            if len(ks) == 1:
+                @pl.when(j == ks[0])
+                def _():
+                    for action in found[1 + ks[0] * chunks + chunk]:
+                        handle(action, my_flip)
+            elif ks:
+                cut = ks[len(ks) // 2]
+                pl.when(j < cut)(lambda: tree(found, [k for k in ks if k < cut]))
+                pl.when(j >= cut)(lambda: tree(found, [k for k in ks if k >= cut]))
+
+        for kind, found in enumerate(slots):
+            if any(1 + k * chunks + chunk in found for k in range(copies)):
+                pl.when(my_kind == kind)(lambda: tree(found, list(range(copies))))
+
     home = (0,) * len(dims)
 
     def start_own(kinds):
         for part, (kind, *_) in enumerate(parts):
             if kind in kinds:
-                launch(part, home, lambda kind: kind[0] == "core")
+                launch(part, home, lambda kind: kind[0] == CORE)
 
     barrier = pltpu.get_barrier_semaphore()
     for k in range(1, flight):
@@ -444,13 +464,15 @@
     load_g.start()
     load_d.start()
     mine = pl.ds(pl.multiple_of(me * tok_count, tok_count), tok_count)
-    own_x = pltpu.make_async_copy(tok_ref, gx.at[mine, :], own_sem.at[0])
-    own_o = pltpu.make_async_copy(og_ref, go.at[mine, :], own_sem.at[1])
+    own_x = pltpu.make_async_copy(tok_ref, gathered.at[me, 0], own_sem.at[0])
+    own_o = pltpu.make_async_copy(og_ref, gathered.at[me, 1], own_sem.at[1])
     own_x.start()
     own_o.start()
+    own_x.wait()
+    own_o.wait()
     pl.semaphore_wait(barrier, greeted)
     run_actions(0)
-    start_own((TOKENS, COTANGENTS))
+    start_own((BLOCK,))
 
     lanes = lax.broadcasted_iota(jnp.int32, (tok_count, routed), 1)
 
@@ -513,13 +535,17 @@
                 if kind in kinds:
                     arrival(part, index).wait_recv()
 
+    def reload_x(group):
+        blocks = pl.ds(pl.multiple_of(group * flight, flight), flight)
+        return pltpu.make_async_copy(gathered.at[blocks, 0], ob, load_sem.at[1])
+
     def load_x(group):
-        rows = pl.ds(pl.multiple_of(group * rows_group, rows_group), rows_group)
-        return pltpu.make_async_copy(gx.at[rows, :], xb, load_sem.at[0])
+        blocks = pl.ds(pl.multiple_of(group * flight, flight), flight)
+        return pltpu.make_async_copy(gathered.at[blocks, 0], xb, load_sem.at[0])
 
     def load_o(group):
-        rows = pl.ds(pl.multiple_of(group * rows_group, rows_group), rows_group)
-        return pltpu.make_async_copy(go.at[rows, :], ob, load_sem.at[1])
+        blocks = pl.ds(pl.multiple_of(group * flight, flight), flight)
+        return pltpu.make_async_copy(gathered.at[blocks, 1], ob, load_sem.at[1])
 
     ranks = lax.broadcasted_iota(jnp.int32, (2 * cap, 2 * tok_count), 0).astype(F32)
 
@@ -534,12 +560,12 @@
         for pair in range(flight // 2):
             picks = pair_rank(group, pair).astype(F32).astype(BF16)
             target[pair * 2 * cap:(pair + 1) * 2 * cap, :] = jnp.dot(
-                picks, source[pair * 2 * tok_count:(pair + 1) * 2 * tok_count, :],
+                picks, source[2 * pair:2 * pair + 2].reshape(2 * tok_count, width),
                 preferred_element_type=F32,
             ).astype(BF16)
 
     def gather_x(group):
-        wait_sibling(group, (TOKENS, COTANGENTS, META))
+        wait_sibling(group, (BLOCK, META))
         load_x(group).start()
         load_o(group).start()
         for pair in range(flight // 2):
@@ -692,14 +718,13 @@
             )
             tg_ref[:, col:col + wide] = total.astype(BF16)
 
-    def router(group):
+    def router(group, held):
         wait_sibling(group, (LOGIT,))
-        load_x(group).wait()
         rows = pl.ds(pl.multiple_of(group * rows_group, rows_group), rows_group)
         grad = lref[rows, :].astype(F32).T.astype(BF16)
         for col in range(0, width, wide):
             rgt[:, col:col + wide] += jnp.dot(
-                grad, xb[:, col:col + wide], preferred_element_type=F32
+                grad, held[:, :, col:col + wide].reshape(rows_group, wide), preferred_element_type=F32
             )
 
     tiles = hidden_units // tile
@@ -716,29 +741,30 @@
         def then(run):
             chunk = spot_now[0]
             spot_now[0] += 1
-            for k in range(copies):
-                run_actions(1 + k * chunks + chunk, j == k)
+            run_steps(j, chunk)
             run()
 
         def first_rows():
-            @pl.when(own)
+            gather_x(group)
+
+            @pl.when(late_half & (j < copies - 1))
             def _():
-                own_x.wait()
-                own_o.wait()
-
-            gather_x(group)
-
-            @pl.when(late_half)
-            def _():
-                load_x(early).start()
+                load_x(second).start()
 
             @pl.when(own)
             def _():
                 load_g.wait()
                 load_d.wait()
 
+        def second_rows():
+            gather_o(group)
+
+            @pl.when(late_half)
+            def _():
+                reload_x(early).start()
+
         then(first_rows)
-        then(lambda: gather_o(group))
+        then(second_rows)
         for index in range(tiles):
             then(functools.partial(gate_tile, index * tile))
             then(functools.partial(up_tile, index * tile))
@@ -753,15 +779,19 @@
 
             @pl.when(late_half)
             def _():
-                router(early)
-                load_x(second).start()
+                reload_x(early).wait()
+                router(early, ob)
 
         def special_late():
             pl.when(j == 0)(send_rows)
 
             @pl.when(late_half)
             def _():
-                router(second)
+                @pl.when(j < copies - 1)
+                def _():
+                    load_x(second).wait()
+
+                router(second, xb)
 
         then(special)
         then(special_late)
@@ -772,8 +802,24 @@
     gu_ref[0] = acc_gu[...].astype(BF16)
     dn_ref[0] = acc_dn[pl.ds(dn_off, dn_rows), :].astype(BF16)
     rout_ref[...] = rgt[...].T
-    for part, js in sorted({key[:2] for key in sites.index}):
-        each(part, js, lambda copy: copy.wait_send())
+    for part, count in sites.shared.items():
+        kind, start, rows, _ = parts[part]
+        if kind == META:
+            sent = mref.at[pl.ds(0, count)]
+        elif kind == LOGIT:
+            sent = lref.at[pl.ds(0, count * tok_count), :]
+        elif kind == BLOCK:
+            sent = gathered.at[pl.ds(0, count)]
+        else:
+            sent = gathered.at[pl.ds(0, count), :, pl.ds(start, rows), :]
+        pltpu.make_async_remote_copy(
+            src_ref=sent, dst_ref=sent, send_sem=send_sem.at[part], recv_sem=recv_sem.at[part, 0],
+            device_id=(d, lax.rem(e + 1, flight)), device_id_type=MESH,
+        ).wait_send()
+    for (part, js, kind), site in sites.index.items():
+        if site >= len(parts):
+            guard, copy = outgoing(part, js, kind)
+            pl.when(guard)(copy.wait_send)
     for k in range(1, flight):
         give_score(k, e).wait_send()
         give_dx(k, e).wait_send()
@@ -817,12 +863,12 @@
     grid = grid_of(n, flight)
     parts = make_parts(grid, tok_count)
     sites = Sites(grid, parts)
-    sizes = [p[2] * width * 2 for p in parts]
+    sizes = [p[2] * width * 4 for p in parts]
     sizes[-2], sizes[-1] = 8 * flight * tok_count, 2 * tok_count * routed
     tiles = hidden // min(hidden, 512)
     base = [1.9, 1.0] + [0.57, 0.57, 0.75] * tiles + [0.75, 0.55]
     chunk_times = [
-        base + ([2.0, 2.0] if j == 0 else [1.6, 0.1] if j < 3 else [0.1, 0.1] if j < n // 2 else [1.3, 1.3])
+        base + ([2.0, 2.0] if j == 0 else [1.6, 0.1] if j < 3 else [0.1, 0.1] if j < n // 2 else [0.8, 0.8])
         for j in range(n)
     ]
     chunks = len(base) + 2
@@ -833,7 +879,7 @@
     hbm = pl.BlockSpec(memory_space=pl.ANY)
     shape = jax.ShapeDtypeStruct
     blocks = n * flight
-    gate_up_grad, down_grad, router_grad, token_grad, _, _ = pl.pallas_call(
+    gate_up_grad, down_grad, router_grad, token_grad, _ = pl.pallas_call(
         functools.partial(
             layer_kernel, n, flight, cap, grid, parts, sites, table, slots, orders, chunks
         ),
@@ -842,16 +888,15 @@
             shape((1, dn_rows, width), BF16),
             shape((width, routed), F32),
             shape((tok_count, width), BF16),
-            shape((blocks * tok_count, width), BF16),
-            shape((blocks * tok_count, width), BF16),
+            shape((blocks, 2, tok_count, width), BF16),
         ),
         in_specs=[vmem] * 5 + [hbm] * 2,
-        out_specs=(vmem,) * 4 + (hbm,) * 2,
+        out_specs=(vmem,) * 4 + (hbm,),
         scratch_shapes=[
             pltpu.VMEM(w_gateup.shape, BF16),
             pltpu.VMEM(w_down.shape, BF16),
-            pltpu.VMEM((flight * tok_count, width), BF16),
-            pltpu.VMEM((flight * tok_count, width), BF16),
+            pltpu.VMEM((flight, tok_count, width), BF16),
+            pltpu.VMEM((flight, tok_count, width), BF16),
             pltpu.VMEM((rows, width), BF16),
             pltpu.VMEM((rows, width), BF16),
             pltpu.VMEM((rows, 128), F32),
@@ -872,7 +917,7 @@
             pltpu.VMEM((rows, routed), F32),
             pltpu.VMEM((flight, cap, routed), F32),
             dma, dma, dma((2,)), dma((2,)),
-            dma((len(sites.index),)), dma((len(parts), blocks)),
+            dma((sites.total,)), dma((len(parts), blocks)),
         ] + [dma((flight - 1,))] * 4,
         compiler_params=pltpu.CompilerParams(
             collective_id=0, has_side_effects=True, vmem_limit_bytes=67_000_000

time: 191 us -> 173 us (0.906)
  Pallas kernels: 190 us -> 172 us
    pallas_call x1, Pallas kernels: 186 us -> 168 us  [per_device(): pl.pallas_call(functools.partial(layer_kernel, n, flight, cap, grid, part...]
where the time goes in v3:
time: 173 us; the launch traced here: 172 us
  Pallas kernels  172 us (99%)
    pallas_call x1, Pallas kernels, per_device(): pl.pallas_call(functools.partial(layer_kernel, n, flight, cap, grid, part...  168 us

profile of v3, /device:TPU:0, one launch (start us, length us, event | category | flops | bytes accessed | tf_op | source)
XLA Modules:
  0.0 172.3 jit_solution(10876669058080781176)
XLA Ops:
  0.6 168.3 %layer.1 = (bf16[1,256,3072]{2,1,0:T(8,128)(2,1)}, bf16[1,192,2048]{2,1,0:T(8,128)(2,1)}, f32[2048,128]{1,0:T(8,128)}, bf16[128,2048]{1,0:T(8,128)(2,1)}, bf16[32,2,128,2048]{3,2,1,0:T(8,128)(2,1)}) custom-call(bf16[128,2048]{1,0:T(8,128)(2,1)} %refs_0_.1, bf16[128,2048]{1,0:T(8,128)(2,1)} %refs_1_.1, bf16[2048,128]{1,0:T(8,128)(2,1)} %refs_2_.1, ...), custom_call_target="tpu_custom_call" | custom-call | tf_op jit(solution)/shard_map/layer/pallas_call | solution.py:882
  168.9 3.4 %finish.1 = (bf16[128,2048]{1,0:T(8,128)(2,1)}, f32[2048,128]{1,0:T(8,128)}, bf16[1,256,3072]{2,1,0:T(8,128)(2,1)}, bf16[1,192,2048]{2,1,0:T(8,128)(2,1)}) custom-call(bf16[128,2048]{1,0:T(8,128)(2,1)} %get-tuple-element.8.refs_0_, f32[2048,128]{1,0:T(8,128)} %get-tuple-element.9.refs_1_, bf16[1,256,3072]{2,1,0:T(8,128)(2,1)} %get-tuple-element.10.refs_2_, ...), custom_call_target="tpu_custom_call" | custom-call | tf_op jit(solution)/shard_map/finish/pallas_call | solution.py:936
